TPU v7x, 256 devices: a whole 4x4x8 slice. The times are simulated.
256 devices in a mesh: prow: 16 (over y, x), pcol: 16 (over z, core).
Axes of the slice: x: 4, y: 4, z: 8, core: 2. Of those that a mesh axis runs over, the one named last changes fastest.
Arguments:
- matrix: float32 [4, 16, 256, 4, 16, 256], P(None, 'prow', None, None, 'pcol'), may hold values from -6 to 6, as said below
- factor: float32 [4, 16, 256, 4, 16, 256], P(None, 'prow', None, None, 'pcol'), may hold values from -3 to 3, as said below
Outputs:
- reduced: float32 [4, 16, 256, 4, 16, 256], P(None, 'prow', None, None, 'pcol')
Inputs may be any that keep to these rules, and one draw needn't show every extreme that they name: Symmetric matrix stored in its lower triangle: every entry above the diagonal is zero. `factor`: lower triangular with diagonal entries between 1 and 3; every entry above the diagonal is zero.
All inputs are finite; a program needn't handle non-finite values.
Results may differ from a plain program's by a relative error of at most 0.0001.
Values sent between devices are 32-bit elements; how exact they have to be, the bound alone decides.
No kernel may reach another device: no remote copies, remote signals or barrier semaphores. Data moves between devices by JAX's collectives and lax.ppermute only.
A program may use at most 128 MiB of HBM per device.

v0:
```python
import jax
import jax.numpy as jnp
from jax import lax
from jax.experimental import pallas as pl
from jax.experimental.pallas import tpu as pltpu
from jax.sharding import Mesh
from jax.sharding import PartitionSpec as P


NB = 256
ROW = ("y", "x")
COL = ("z", "core")
SLABS = 8
SLAB = NB // SLABS


NT = (((1,), (1,)), ((), ()))
NN = (((1,), (0,)), ((), ()))


def full(left, right, dims=NT):
    return lax.dot_general(left, right, dims, precision=lax.Precision.HIGHEST, preferred_element_type=jnp.float32)


def split(value):
    high = value.astype(jnp.bfloat16)
    return high, (value - high.astype(jnp.float32)).astype(jnp.bfloat16)


def three(left, right):
    def dot(a, b):
        return lax.dot_general(a, b, NT, preferred_element_type=jnp.float32)

    return dot(left[0], right[0]) + dot(left[0], right[1]) + dot(left[1], right[0])


def pack_kernel(place, matrix, factor, *rest):
    pieces, (buffer, sems) = rest[:SLABS], rest[SLABS:]

    @pl.when(place[2] == 0)
    def _():
        copies = {}
        for tile in range(4):
            for m, source in enumerate((matrix, factor)):
                rows = pl.ds(tile * 8 * NB, 8 * NB)
                copies[tile, m] = pltpu.make_async_copy(source.at[rows], buffer.at[m, rows], sems.at[m * 4 + tile])
                copies[tile, m].start()
        for tile in range(4):
            for m in range(2):
                copies[tile, m].wait()
                for half in range(2):
                    for slab in range(SLABS):
                        value = buffer[m, pl.ds((tile * NB + slab * SLAB) * 8 + half, SLAB, stride=8), :]
                        pieces[slab][pl.ds(((m * 4 + tile) * 2 + half) * SLAB, SLAB), :] = value


def pack(place, matrix, factor):
    return pl.pallas_call(
        pack_kernel,
        in_specs=[pl.BlockSpec(memory_space=pltpu.SMEM)] + [pl.BlockSpec(memory_space=pl.ANY)] * 2,
        out_specs=[pl.BlockSpec(memory_space=pltpu.VMEM)] * SLABS,
        out_shape=[jax.ShapeDtypeStruct((16 * SLAB, 128), jnp.float32)] * SLABS,
        scratch_shapes=[pltpu.VMEM((2, 8192, 128), jnp.float32), pltpu.SemaphoreType.DMA((8,))],
        compiler_params=pltpu.CompilerParams(vmem_limit_bytes=40 * 2**20),
        name="pack",
    )(place, matrix, factor)


def iotas():
    return (
        lax.broadcasted_iota(jnp.int32, (NB, NB), 0),
        lax.broadcasted_iota(jnp.int32, (NB, NB), 1),
    )


def inverses(lowers, rows, cols):
    eye = rows == cols
    pair = (rows // 2 == cols // 2) & (rows > cols)
    first = []
    for lower in lowers:
        down = 1.0 / jnp.sum(jnp.where(eye, lower, 0.0), axis=1, keepdims=True)
        across = 1.0 / jnp.sum(jnp.where(eye, lower, 0.0), axis=0, keepdims=True)
        first.append(jnp.where(eye, down, 0.0) - jnp.where(pair, lower * down * across, 0.0))

    def double(level, values):
        size = jnp.right_shift(rows, level) - jnp.right_shift(cols, level)
        band = (size == 1) & (jnp.right_shift(rows, level + 1) == jnp.right_shift(cols, level + 1))
        blocks = [full(value, jnp.where(band, lower, 0.0), NN) for value, lower in zip(values, lowers)]
        return tuple(value - full(block, value, NN) for value, block in zip(values, blocks))

    return lax.fori_loop(1, 8, double, tuple(first))


def head_kernel(place, *rest):
    parts, (out, head, done, sems) = rest[:9], rest[9:]
    z = place[2]
    for offset, part in zip((0, -1, 1, -2, 2, -3, 3), parts):
        head[(z + offset + SLABS) % SLABS] = part[...]
    far = (z + 4) % SLABS
    head[far, :6] = parts[7][...]
    head[far, 6:] = parts[8][...]
    rows, cols = iotas()
    eye = rows == cols

    def tile(k):
        return jnp.concatenate([head[:, 2 * k + half].reshape(NB, 128) for half in range(2)], axis=1)

    a00, l00, a10, low, a11, l11 = (tile(k) for k in range(6))
    inv0, inv1 = inverses((l00, l11), rows, cols)
    part = full(full(inv0, jnp.where(eye, 0.5 * a00, a00), NN), inv0)
    core0 = part + part.T
    half0 = full(a10, inv0) - 0.5 * full(low, core0)
    inner = jnp.where(eye, 0.5 * a11, a11) - full(half0, low)
    part = full(full(inv1, inner, NN), inv1)
    core1 = part + part.T
    copies = []
    for k, value in enumerate((inv0, core0, inv1, core1, half0, low)):
        done[k] = value
        copies.append(pltpu.make_async_copy(done.at[k], out.at[k], sems.at[k]))
        copies[k].start()
    for copy in copies:
        copy.wait()


def head_math(place, parts):
    parts = [part.reshape(-1, SLAB, 128) for part in parts]
    return pl.pallas_call(
        head_kernel,
        in_specs=[pl.BlockSpec(memory_space=pltpu.SMEM)] + [pl.BlockSpec(memory_space=pltpu.VMEM)] * 9,
        out_specs=pl.BlockSpec(memory_space=pltpu.HBM),
        out_shape=pltpu.HBM((6, NB, NB), jnp.float32),
        scratch_shapes=[
            pltpu.VMEM((SLABS, 12, SLAB, 128), jnp.float32),
            pltpu.VMEM((6, NB, NB), jnp.float32),
            pltpu.SemaphoreType.DMA((6,)),
        ],
        compiler_params=pltpu.CompilerParams(vmem_limit_bytes=16 * 2**20),
        name="head",
    )(place, *parts)


def main_kernel(place, raw_far, local_far, head_far, *rest):
    rows_in, rest = rest[:14], rest[14:]
    out, raw_row, raw_col, local, head, col_hi, col_lo, head_hi, head_lo, sems = rest
    step = pl.program_id(0)
    p = place[0]
    c = place[1]
    z = place[2]
    core = c % 2

    def load_local(tile):
        return pltpu.make_async_copy(local_far.at[pl.ds(tile * 2048, 2048)], local.at[tile], sems.at[tile])

    def read(raw, core, m, tile):
        return jnp.concatenate([raw[:, core, m, tile, half].reshape(NB, 128) for half in range(2)], axis=1)

    def panels(raw, tile):
        def heads(k):
            return head_hi[k], head_lo[k]

        a0, a1 = read(raw, 0, 0, tile), read(raw, 1, 0, tile)
        f0, f1 = split(read(raw, 0, 1, tile)), split(read(raw, 1, 1, tile))
        p0 = three(f0, heads(1))
        half0 = three(split(a0), heads(0)) - 0.5 * p0
        g0 = split(half0)
        a1 = a1 - three(g0, heads(5)) - three(f0, heads(4))
        p1 = three(f1, heads(3))
        half1 = three(split(a1), heads(2)) - 0.5 * p1
        g1 = split(half1)
        return g0, f0, g1, f1, half0 - 0.5 * p0, half1 - 0.5 * p1

    @pl.when(step == 0)
    def _():
        load_col = pltpu.make_async_copy(raw_far, raw_col, sems.at[4])
        load_head = pltpu.make_async_copy(head_far, head, sems.at[5])
        load_head.start()
        load_col.start()
        for tile in range(4):
            load_local(tile).start()
        for which, side in ((0, core), (1, 1 - core)):
            for k, offset in enumerate((0, -1, 1, -2, 2, -3, 3)):
                part = rows_in[k] if which == 0 else rows_in[9 + (k + 1) // 2]
                at = 0 if which == 0 or k == 0 else (k + 1) % 2
                raw_row[(z + offset + SLABS) % SLABS, side] = part[at]
            far = (z + 4) % SLABS
            for m in range(2):
                raw_row[far, side, m] = rows_in[7 + m][0] if which == 0 else rows_in[13][m]
        load_head.wait()
        for k in range(6):
            head_hi[k], head_lo[k] = split(head[k])
        load_col.wait()

        def one(tile, carry):
            g0, f0, g1, f1, _, _ = panels(raw_col, tile)
            for k, (hi, lo) in enumerate((f0, g0, f1, g1)):
                col_hi[tile, :, k * NB : (k + 1) * NB] = hi
                col_lo[tile, :, k * NB : (k + 1) * NB] = lo
            return carry

        lax.fori_loop(0, 4, one, 0)

    g0, f0, g1, f1, done0, done1 = panels(raw_row, step)
    load_local(step).wait()
    row_hi = jnp.concatenate([g0[0], f0[0], g1[0], f1[0]], axis=1)
    row_lo = jnp.concatenate([g0[1], f0[1], g1[1], f1[1]], axis=1)
    rows, cols = iotas()

    def put(tile, value):
        for half in range(2):
            out[pl.ds(tile * 2 + half, NB, stride=8), :] = value[:, half * 128 : (half + 1) * 128]

    def get(tile):
        return jnp.concatenate([local[step, pl.ds(tile * 2 + half, NB, stride=8), :] for half in range(2)], axis=1)

    def update(tile, carry):
        below = (step > tile) | ((step == tile) & (p > c))
        same = (step == tile) & (p == c)
        ours = (below | same) & ((tile > 0) | (c > 1))

        @pl.when(ours)
        def _():
            change = three((row_hi, row_lo), (col_hi[tile], col_lo[tile]))
            keep = jnp.logical_or(below, rows >= cols)
            put(tile, get(tile) - jnp.where(keep, change, 0.0))

        @pl.when(jnp.logical_not(ours))
        def _():
            put(tile, get(tile))

        return carry

    lax.fori_loop(0, 4, update, 0)
    top = step * 16 + p
    for block, done in enumerate((done0, done1)):

        @pl.when((c == block) & (top > block))
        def _():
            put(0, done)

        @pl.when((c == block) & (top == block))
        def _():
            put(0, jnp.where(rows >= cols, head[2 * block + 1], 0.0))


def main_math(place, rows, raw_col, head, local):
    raw = (SLABS, 2, 2, 4, 2, SLAB, 128)
    vmem = pl.BlockSpec(memory_space=pltpu.VMEM)
    hbm = pl.BlockSpec(memory_space=pltpu.HBM)
    whole = [rows[k].reshape(-1, 2, 4, 2, SLAB, 128) for k in (0, 1, 2, 3, 4, 5, 6)]
    halves = [rows[k].reshape(1, 4, 2, SLAB, 128) for k in (7, 8)]
    crossed = [rows[k].reshape(-1, 2, 4, 2, SLAB, 128) for k in (9, 10, 11, 12)] + [rows[13].reshape(2, 4, 2, SLAB, 128)]
    return pl.pallas_call(
        main_kernel,
        grid=(4,),
        in_specs=[pl.BlockSpec(memory_space=pltpu.SMEM), hbm, hbm, hbm] + [vmem] * 14,
        out_specs=pl.BlockSpec((2048, 128), lambda i: (i, 0)),
        out_shape=jax.ShapeDtypeStruct((8192, 128), jnp.float32),
        scratch_shapes=[
            pltpu.VMEM(raw, jnp.float32),
            pltpu.VMEM(raw, jnp.float32),
            pltpu.VMEM((4, 2048, 128), jnp.float32),
            pltpu.VMEM((6, NB, NB), jnp.float32),
            pltpu.VMEM((4, NB, 4 * NB), jnp.bfloat16),
            pltpu.VMEM((4, NB, 4 * NB), jnp.bfloat16),
            pltpu.VMEM((6, NB, NB), jnp.bfloat16),
            pltpu.VMEM((6, NB, NB), jnp.bfloat16),
            pltpu.SemaphoreType.DMA((6,)),
        ],
        compiler_params=pltpu.CompilerParams(vmem_limit_bytes=32 * 2**20),
        name="main",
    )(place, far(raw_col.reshape(raw)), far(local), far(head), *whole, *halves, *crossed)


def shift(value, axis, size, by):
    return lax.ppermute(value, axis, [(i, (i + by) % size) for i in range(size)])


def ring8(value):
    up1, down1 = shift(value, "z", 8, 1), shift(value, "z", 8, -1)
    up2, down2 = shift(up1, "z", 8, 1), shift(down1, "z", 8, -1)
    up3, down3 = shift(up2, "z", 8, 1), shift(down2, "z", 8, -1)
    half = value.shape[0] // 2
    up4, down4 = shift(up3[:half], "z", 8, 1), shift(down3[half:], "z", 8, -1)
    return [value, up1, down1, up2, down2, up3, down3, up4, down4]


def far(value):
    return pltpu.with_memory_space_constraint(value, pltpu.HBM)


def crossed(*values):
    return lax.ppermute(jnp.concatenate(values, 0), "core", [(0, 1), (1, 0)])


def device(matrix, factor):
    x, y, z, core = (lax.axis_index(name) for name in ("x", "y", "z", "core"))
    p = lax.axis_index(ROW)
    c = lax.axis_index(COL)
    place = jnp.stack([p, c, z])
    local = matrix.reshape(8192, 128)
    pieces = pack(place, local, factor.reshape(8192, 128))
    order = (4, 1, 7, 2, 6, 3, 5)
    got = [lax.ppermute(pieces[k], "z", [(0, k)]) for k in order]
    total = got[0]
    for value in got[1:]:
        total = total + value
    mine = jnp.where(z == 0, pieces[0], total)
    swapped = lax.ppermute(mine, ROW + COL, [(r * 16 + j, j * 16 + r) for r in range(16) for j in range(16)])
    top = mine.reshape(2, 4, 2 * SLAB, 128)[:, 0].reshape(4 * SLAB, 128)
    other = lax.ppermute(top, "core", [(0, 1), (1, 0)])
    both = jnp.where(core == 0, jnp.concatenate([top, other], 0), jnp.concatenate([other, top], 0))
    across = lax.ppermute(both, ROW, [(0, 1), (1, 0)])
    zero, one = jnp.where(p == 0, both, across), jnp.where(p == 0, across, both)
    head = jnp.concatenate([zero[: 4 * SLAB], one], 0)
    sent = lax.ppermute(head, ROW, [(0, 3), (1, 2)])
    head = jnp.where(x < 2, head, sent)
    sent1 = lax.ppermute(head, "y", [(0, 1)])
    sent3 = lax.ppermute(head, "y", [(0, 3)])
    swapped, sent1, sent3 = lax.optimization_barrier((swapped, sent1, sent3))
    raw_col = lax.all_gather(swapped, ROW)
    sent2 = lax.ppermute(sent1, "y", [(1, 2)])
    head = jnp.where(y == 0, head, jnp.where(y == 1, sent1, jnp.where(y == 2, sent2, sent3)))
    head = head_math(place, ring8(head))
    rows = ring8(mine)
    rows = rows + [crossed(*rows[k : k + 2]) if k else crossed(rows[0]) for k in (0, 1, 3, 5, 7)]
    return main_math(place, rows, raw_col, head, local).reshape(matrix.shape)


def solution(mesh):
    torus = Mesh(mesh.devices.reshape(4, 4, 8, 2), ("y", "x", "z", "core"))
    spec = P(None, ROW, None, None, COL, None)
    return jax.shard_map(device, mesh=torus, in_specs=(spec, spec), out_specs=spec, check_vma=False)
```

profile of v0, /device:TPU:31, one launch (start us, length us, event | category | flops | bytes accessed | tf_op | source)
XLA Modules:
  0.0 174.5 jit_solution(12173374462169780668)
XLA Ops:
  6.5 0.1 pad_add_fusion.place
  6.6 2.2 %copy-done = f32[4,1,256,4,1,256]{5,4,3,2,1,0:T(1,128)S(1)} copy-done((f32[4,1,256,4,1,256]{5,4,3,2,1,0:T(1,128)S(1)}, f32[4,1,256,4,1,256]{5,4,3,2,1,0:T(1,128)}, u32[]{:S(2)}) %copy-start) | copy-done | bytes 4194328
  8.8 2.2 %copy-done.1 = f32[4,1,256,4,1,256]{5,4,3,2,1,0:T(1,128)S(1)} copy-done((f32[4,1,256,4,1,256]{5,4,3,2,1,0:T(1,128)S(1)}, f32[4,1,256,4,1,256]{5,4,3,2,1,0:T(1,128)}, u32[]{:S(2)}) %copy-start.1) | copy-done | bytes 4194328
  11.0 1.7 pack.1
  12.7 7.8 %collective-permute-start = (f32[512,128]{1,0:T(8,128)S(1)}, f32[512,128]{1,0:T(8,128)S(1)}, u32[]{:S(2)}, u32[]{:S(2)}) collective-permute-start(f32[512,128]{1,0:T(8,128)S(1)} %get-tuple-element.17), channel_id=1, source_target_pairs={{0,8},{1,9},{16,24},{17,25},{32,40},{33,41},{48,56},{49,57},{64,72... | collective-permute-start | bytes 786440 | tf_op jit(solution)/shard_map/ppermute | solution.py:303
  20.5 1.3 collective-permute-start.1
  21.8 1.3 collective-permute-start.2
  23.1 1.3 collective-permute-start.3
  24.4 1.3 collective-permute-start.4
  25.7 1.3 collective-permute-start.5
  27.0 4.0 %collective-permute-done.1 = f32[512,128]{1,0:T(8,128)S(1)} collective-permute-done((f32[512,128]{1,0:T(8,128)S(1)}, f32[512,128]{1,0:T(8,128)S(1)}, u32[]{:S(2)}, u32[]{:S(2)}) %collective-permute-start.1) | collective-permute-done | bytes 262176 | tf_op jit(solution)/shard_map/ppermute | solution.py:303
  31.0 1.3 collective-permute-start.6
  32.3 4.3 %collective-permute-done.3 = f32[512,128]{1,0:T(8,128)S(1)} collective-permute-done((f32[512,128]{1,0:T(8,128)S(1)}, f32[512,128]{1,0:T(8,128)S(1)}, u32[]{:S(2)}, u32[]{:S(2)}) %collective-permute-start.3) | collective-permute-done | bytes 262176 | tf_op jit(solution)/shard_map/ppermute | solution.py:303
  36.7 5.6 %collective-permute-done.5 = f32[512,128]{1,0:T(8,128)S(1)} collective-permute-done((f32[512,128]{1,0:T(8,128)S(1)}, f32[512,128]{1,0:T(8,128)S(1)}, u32[]{:S(2)}, u32[]{:S(2)}) %collective-permute-start.5) | collective-permute-done | bytes 262176 | tf_op jit(solution)/shard_map/ppermute | solution.py:303
  42.3 0.0 collective-permute-done.6
  42.3 0.1 add_select_fusion
  42.4 1.6 collective-permute-start.8
  44.0 0.9 collective-permute-done.8
  44.9 0.7 collective-permute-start.9
  45.7 0.7 collective-permute-start.10
  46.4 1.9 %collective-permute-start.7 = (f32[512,128]{1,0:T(8,128)S(1)}, f32[512,128]{1,0:T(8,128)S(1)}, u32[]{:S(2)}, u32[]{:S(2)}) collective-permute-start(f32[512,128]{1,0:T(8,128)S(1)} %add_select_fusion), channel_id=1, source_target_pairs={{0,0},{1,16},{2,32},{3,48},{4,64},{5,80},{6,96},{7,112},{8,128},{9... | collective-permute-start | bytes 786440 | tf_op jit(solution)/shard_map/ppermute | solution.py:308
  48.3 1.3 collective-permute-start.12
  49.6 0.7 collective-permute-start.11
  50.3 32.1 %collective-permute-done.7 = f32[512,128]{1,0:T(8,128)S(1)} collective-permute-done((f32[512,128]{1,0:T(8,128)S(1)}, f32[512,128]{1,0:T(8,128)S(1)}, u32[]{:S(2)}, u32[]{:S(2)}) %collective-permute-start.7) | collective-permute-done | bytes 262176 | tf_op jit(solution)/shard_map/ppermute | solution.py:308
  82.4 0.0 collective-permute-done.12
  82.4 0.0 collective-permute-done.11
  82.4 0.7 copy-done.6
  83.1 0.0 all-gather.3.cloned.1.call-update
  83.1 0.1 collective-permute-start.23
  83.2 1.5 collective-permute-start.22
  84.7 0.7 collective-permute-start.13
  85.4 4.8 %collective-permute-done.23 = f32[512,128]{1,0:T(8,128)S(1)} collective-permute-done((f32[512,128]{1,0:T(8,128)S(1)}, f32[512,128]{1,0:T(8,128)S(1)}, u32[]{:S(2)}, u32[]{:S(2)}) %collective-permute-start.23) | collective-permute-done | bytes 262176 | tf_op jit(solution)/shard_map/ppermute | solution.py:275
  90.2 1.5 collective-permute-start.25
  91.7 0.0 collective-permute-done.22
  91.7 0.0 collective-permute-start.24
  91.7 0.0 collective-permute-done.13
  91.7 2.7 %collective-permute-start.15 = (f32[384,128]{1,0:T(8,128)S(1)}, f32[384,128]{1,0:T(8,128)S(1)}, u32[]{:S(2)}, u32[]{:S(2)}) collective-permute-start(f32[384,128]{1,0:T(8,128)S(1)} %select_select_fusion), channel_id=1, source_target_pairs={{0,14},{2,0},{4,2},{6,4},{8,6},{10,8},{12,10},{14,12},{1,15},{3,1}... | collective-permute-start | bytes 589832 | tf_op jit(solution)/shard_map/ppermute | solution.py:275
  94.5 1.9 %collective-permute-done.25 = f32[512,128]{1,0:T(8,128)S(1)} collective-permute-done((f32[512,128]{1,0:T(8,128)S(1)}, f32[512,128]{1,0:T(8,128)S(1)}, u32[]{:S(2)}, u32[]{:S(2)}) %collective-permute-start.25) | collective-permute-done | bytes 262176 | tf_op jit(solution)/shard_map/ppermute | solution.py:275
  96.4 3.0 %collective-permute-start.27 = (f32[512,128]{1,0:T(8,128)S(1)}, f32[512,128]{1,0:T(8,128)S(1)}, u32[]{:S(2)}, u32[]{:S(2)}) collective-permute-start(f32[512,128]{1,0:T(8,128)S(1)} %collective-permute-done.25), channel_id=1, source_target_pairs={{0,14},{2,0},{4,2},{6,4},{8,6},{10,8},{12,10},{14,12},{1,15},{3,1}... | collective-permute-start | bytes 786440 | tf_op jit(solution)/shard_map/ppermute | solution.py:275
  99.4 1.2 collective-permute-done.15
  100.6 3.0 %collective-permute-start.17 = (f32[384,128]{1,0:T(8,128)S(1)}, f32[384,128]{1,0:T(8,128)S(1)}, u32[]{:S(2)}, u32[]{:S(2)}) collective-permute-start(f32[384,128]{1,0:T(8,128)S(1)} %collective-permute-done.15), channel_id=1, source_target_pairs={{0,14},{2,0},{4,2},{6,4},{8,6},{10,8},{12,10},{14,12},{1,15},{3,1}... | collective-permute-start | bytes 589832 | tf_op jit(solution)/shard_map/ppermute | solution.py:275
  103.6 0.0 collective-permute-done.14
  103.6 0.0 collective-permute-start.16
  103.6 0.0 collective-permute-done.24
  103.6 0.1 collective-permute-start.26
  103.7 4.6 %collective-permute-start.31 = (f32[1024,128]{1,0:T(8,128)S(1)}, f32[1024,128]{1,0:T(8,128)S(1)}, u32[]{:S(2)}, u32[]{:S(2)}) collective-permute-start(f32[1024,128]{1,0:T(8,128)S(1)} %pad_maximum_fusion), channel_id=1, source_target_pairs={{0,1},{1,0},{2,3},{3,2},{4,5},{5,4},{6,7},{7,6},{8,9},{9,8},{10,11... | collective-permute-start | bytes 1572872 | tf_op jit(solution)/shard_map/ppermute | solution.py:292
  108.3 0.0 collective-permute-done.27
  108.3 3.0 %collective-permute-start.29 = (f32[256,128]{1,0:T(8,128)S(1)}, f32[256,128]{1,0:T(8,128)S(1)}, u32[]{:S(2)}, u32[]{:S(2)}) collective-permute-start(f32[256,128]{1,0:T(8,128)S(1)} %slice.30), channel_id=1, source_target_pairs={{0,14},{2,0},{4,2},{6,4},{8,6},{10,8},{12,10},{14,12},{1,15},{3,1}... | collective-permute-start | bytes 393224 | tf_op jit(solution)/shard_map/ppermute | solution.py:275
  111.3 1.7 collective-permute-start.19
  113.0 5.1 %collective-permute-start.32 = (f32[1024,128]{1,0:T(8,128)S(1)}, f32[1024,128]{1,0:T(8,128)S(1)}, u32[]{:S(2)}, u32[]{:S(2)}) collective-permute-start(f32[1024,128]{1,0:T(8,128)S(1)} %pad_maximum_fusion.1), channel_id=1, source_target_pairs={{0,1},{1,0},{2,3},{3,2},{4,5},{5,4},{6,7},{7,6},{8,9},{9,8},{10,11... | collective-permute-start | bytes 1572872 | tf_op jit(solution)/shard_map/ppermute | solution.py:292
  118.2 0.1 collective-permute-start.33
  118.4 0.1 collective-permute-start.28
  118.5 1.1 collective-permute-done.18
  119.6 1.6 collective-permute-start.21
  121.2 2.7 %collective-permute-done.28 = f32[256,128]{1,0:T(8,128)S(1)} collective-permute-done((f32[256,128]{1,0:T(8,128)S(1)}, f32[256,128]{1,0:T(8,128)S(1)}, u32[]{:S(2)}, u32[]{:S(2)}) %collective-permute-start.28) | collective-permute-done | bytes 131104 | tf_op jit(solution)/shard_map/ppermute | solution.py:275
  123.9 2.3 %collective-permute-start.30 = (f32[512,128]{1,0:T(8,128)S(1)}, f32[512,128]{1,0:T(8,128)S(1)}, u32[]{:S(2)}, u32[]{:S(2)}) collective-permute-start(f32[512,128]{1,0:T(8,128)S(1)} %add_select_fusion), channel_id=1, source_target_pairs={{0,1},{1,0},{2,3},{3,2},{4,5},{5,4},{6,7},{7,6},{8,9},{9,8},{10,11... | collective-permute-start | bytes 786440 | tf_op jit(solution)/shard_map/ppermute | solution.py:292
  126.2 5.1 %collective-permute-done.20 = f32[192,128]{1,0:T(8,128)S(1)} collective-permute-done((f32[192,128]{1,0:T(8,128)S(1)}, f32[192,128]{1,0:T(8,128)S(1)}, u32[]{:S(2)}, u32[]{:S(2)}) %collective-permute-start.20) | collective-permute-done | bytes 98336 | tf_op jit(solution)/shard_map/ppermute | solution.py:275
  131.3 2.1 %collective-permute-start.34 = (f32[512,128]{1,0:T(8,128)S(1)}, f32[512,128]{1,0:T(8,128)S(1)}, u32[]{:S(2)}, u32[]{:S(2)}) collective-permute-start(f32[512,128]{1,0:T(8,128)S(1)} %pad_maximum_fusion.3), channel_id=1, source_target_pairs={{0,1},{1,0},{2,3},{3,2},{4,5},{5,4},{6,7},{7,6},{8,9},{9,8},{10,11... | collective-permute-start | bytes 786440 | tf_op jit(solution)/shard_map/ppermute | solution.py:292
  133.4 13.8 %head.1.head_far = f32[6,256,256]{2,1,0:T(8,128)} custom-call(s32[3]{0:T(128)S(1)} %pad_add_fusion.place, f32[12,32,128]{2,1,0:T(8,128)S(1)} %bitcast.43, f32[12,32,128]{2,1,0:T(8,128)S(1)} %bitcast.54, f32[12,32,128]{2,1,0:T(8,128)S(1)} %bitcast.53, f32[12,32,128]{2,1,0:T(8,128)S(1)} %bitcast.56, f32[12,32,128]{2,1,0:T(8,128)S(1)} %bitcast.55, ...), custom_call_target="tpu_custom_call" | custom-call | tf_op jit(solution)/shard_map/head/pallas_call | solution.py:127
  147.2 0.7 copy-done.4
  147.9 0.8 copy-done.2
  148.7 1.0 copy-done.3
  149.8 0.9 copy-done.5
  150.7 16.9 %main.1 = f32[8192,128]{1,0:T(8,128)} custom-call(s32[3]{0:T(128)S(1)} %pad_add_fusion.place, f32[8,2,2,4,2,32,128]{6,5,4,3,2,1,0:T(8,128)} %bitcast.59, f32[8192,128]{1,0:T(8,128)} %bitcast.32, f32[6,256,256]{2,1,0:T(8,128)} %head.1.head_far, f32[1,2,4,2,32,128]{5,4,3,2,1,0:T(8,128)S(1)} %bitcast.38, f32[1,2,4,2,32,128]{5,4,3,2,1,0:T(8,128)S(1)} %bitcast.40, ...), custom_call_target="tpu_custom_call" | custom-call | tf_op jit(solution)/shard_map/main/pallas_call | solution.py:252
  (43 shorter events, 0.3 us)
Async XLA Ops:
  6.5 142.2 %all-gather.3.cloned.1.call-start = ((), (), s32[]{:S(2)}) async-start(), calls=%async_computation | async-start | bytes 4456448 | tf_op jit(solution)/shard_map/all_gather | solution.py:320
  6.6 2.2 %copy-start = (f32[4,1,256,4,1,256]{5,4,3,2,1,0:T(1,128)S(1)}, f32[4,1,256,4,1,256]{5,4,3,2,1,0:T(1,128)}, u32[]{:S(2)}) copy-start(f32[4,1,256,4,1,256]{5,4,3,2,1,0:T(1,128)} %param.2) | copy-start | bytes 12582916
  8.8 2.2 %copy-start.1 = (f32[4,1,256,4,1,256]{5,4,3,2,1,0:T(1,128)S(1)}, f32[4,1,256,4,1,256]{5,4,3,2,1,0:T(1,128)}, u32[]{:S(2)}) copy-start(f32[4,1,256,4,1,256]{5,4,3,2,1,0:T(1,128)} %param.3) | copy-start | bytes 12582916
  12.7 13.1 %collective-permute-start = (f32[512,128]{1,0:T(8,128)S(1)}, f32[512,128]{1,0:T(8,128)S(1)}, u32[]{:S(2)}, u32[]{:S(2)}) collective-permute-start(f32[512,128]{1,0:T(8,128)S(1)} %get-tuple-element.17), channel_id=1, source_target_pairs={{0,8},{1,9},{16,24},{17,25},{32,40},{33,41},{48,56},{49,57},{64,72... | collective-permute-start | bytes 786440 | tf_op jit(solution)/shard_map/ppermute | solution.py:303
  20.5 10.6 %collective-permute-start.1 = (f32[512,128]{1,0:T(8,128)S(1)}, f32[512,128]{1,0:T(8,128)S(1)}, u32[]{:S(2)}, u32[]{:S(2)}) collective-permute-start(f32[512,128]{1,0:T(8,128)S(1)} %get-tuple-element.18), channel_id=1, source_target_pairs={{0,2},{1,3},{16,18},{17,19},{32,34},{33,35},{48,50},{49,51},{64,66... | collective-permute-start | bytes 786440 | tf_op jit(solution)/shard_map/ppermute | solution.py:303
  21.8 10.6 %collective-permute-start.2 = (f32[512,128]{1,0:T(8,128)S(1)}, f32[512,128]{1,0:T(8,128)S(1)}, u32[]{:S(2)}, u32[]{:S(2)}) collective-permute-start(f32[512,128]{1,0:T(8,128)S(1)} %get-tuple-element.19), channel_id=1, source_target_pairs={{0,14},{1,15},{16,30},{17,31},{32,46},{33,47},{48,62},{49,63},{64,... | collective-permute-start | bytes 786440 | tf_op jit(solution)/shard_map/ppermute | solution.py:303
  23.1 13.6 %collective-permute-start.3 = (f32[512,128]{1,0:T(8,128)S(1)}, f32[512,128]{1,0:T(8,128)S(1)}, u32[]{:S(2)}, u32[]{:S(2)}) collective-permute-start(f32[512,128]{1,0:T(8,128)S(1)} %get-tuple-element.20), channel_id=1, source_target_pairs={{0,4},{1,5},{16,20},{17,21},{32,36},{33,37},{48,52},{49,53},{64,68... | collective-permute-start | bytes 786440 | tf_op jit(solution)/shard_map/ppermute | solution.py:303
  24.4 12.3 %collective-permute-start.4 = (f32[512,128]{1,0:T(8,128)S(1)}, f32[512,128]{1,0:T(8,128)S(1)}, u32[]{:S(2)}, u32[]{:S(2)}) collective-permute-start(f32[512,128]{1,0:T(8,128)S(1)} %get-tuple-element.21), channel_id=1, source_target_pairs={{0,12},{1,13},{16,28},{17,29},{32,44},{33,45},{48,60},{49,61},{64,... | collective-permute-start | bytes 786440 | tf_op jit(solution)/shard_map/ppermute | solution.py:303
  25.7 16.5 %collective-permute-start.5 = (f32[512,128]{1,0:T(8,128)S(1)}, f32[512,128]{1,0:T(8,128)S(1)}, u32[]{:S(2)}, u32[]{:S(2)}) collective-permute-start(f32[512,128]{1,0:T(8,128)S(1)} %get-tuple-element.22), channel_id=1, source_target_pairs={{0,6},{1,7},{16,22},{17,23},{32,38},{33,39},{48,54},{49,55},{64,70... | collective-permute-start | bytes 786440 | tf_op jit(solution)/shard_map/ppermute | solution.py:303
  31.0 11.2 %collective-permute-start.6 = (f32[512,128]{1,0:T(8,128)S(1)}, f32[512,128]{1,0:T(8,128)S(1)}, u32[]{:S(2)}, u32[]{:S(2)}) collective-permute-start(f32[512,128]{1,0:T(8,128)S(1)} %get-tuple-element.23), channel_id=1, source_target_pairs={{0,10},{1,11},{16,26},{17,27},{32,42},{33,43},{48,58},{49,59},{64,... | collective-permute-start | bytes 786440 | tf_op jit(solution)/shard_map/ppermute | solution.py:303
  42.4 2.5 %collective-permute-start.8 = (f32[128,128]{1,0:T(8,128)S(1)}, f32[128,128]{1,0:T(8,128)S(1)}, u32[]{:S(2)}, u32[]{:S(2)}) collective-permute-start(f32[128,128]{1,0:T(8,128)S(1)} %bitcast.60), channel_id=1, source_target_pairs={{0,1},{1,0},{2,3},{3,2},{4,5},{5,4},{6,7},{7,6},{8,9},{9,8},{10,11... | collective-permute-start | bytes 196616 | tf_op jit(solution)/shard_map/ppermute | solution.py:310
  44.9 0.7 collective-permute-start.9
  45.7 2.6 %collective-permute-start.10 = (f32[384,128]{1,0:T(8,128)S(1)}, f32[384,128]{1,0:T(8,128)S(1)}, u32[]{:S(2)}, u32[]{:S(2)}) collective-permute-start(f32[384,128]{1,0:T(8,128)S(1)} %pad_maximum_fusion.4), channel_id=1, source_target_pairs={{0,48},{16,32},{1,49},{17,33},{2,50},{18,34},{3,51},{19,35},{4,52}... | collective-permute-start | bytes 589832 | tf_op jit(solution)/shard_map/ppermute | solution.py:315
  46.4 36.1 %collective-permute-start.7 = (f32[512,128]{1,0:T(8,128)S(1)}, f32[512,128]{1,0:T(8,128)S(1)}, u32[]{:S(2)}, u32[]{:S(2)}) collective-permute-start(f32[512,128]{1,0:T(8,128)S(1)} %add_select_fusion), channel_id=1, source_target_pairs={{0,0},{1,16},{2,32},{3,48},{4,64},{5,80},{6,96},{7,112},{8,128},{9... | collective-permute-start | bytes 786440 | tf_op jit(solution)/shard_map/ppermute | solution.py:308
  48.3 34.1 %collective-permute-start.12 = (f32[384,128]{1,0:T(8,128)S(1)}, f32[384,128]{1,0:T(8,128)S(1)}, u32[]{:S(2)}, u32[]{:S(2)}) collective-permute-start(f32[384,128]{1,0:T(8,128)S(1)} %broadcast_select_fusion), channel_id=1, source_target_pairs={{0,192},{1,193},{2,194},{3,195},{4,196},{5,197},{6,198},{7,199},{8... | collective-permute-start | bytes 589832 | tf_op jit(solution)/shard_map/ppermute | solution.py:318
  49.6 32.8 %collective-permute-start.11 = (f32[384,128]{1,0:T(8,128)S(1)}, f32[384,128]{1,0:T(8,128)S(1)}, u32[]{:S(2)}, u32[]{:S(2)}) collective-permute-start(f32[384,128]{1,0:T(8,128)S(1)} %broadcast_select_fusion), channel_id=1, source_target_pairs={{0,64},{1,65},{2,66},{3,67},{4,68},{5,69},{6,70},{7,71},{8,72},{9,... | collective-permute-start | bytes 589832 | tf_op jit(solution)/shard_map/ppermute | solution.py:317
  82.4 0.7 copy-start.6
  83.1 7.0 %collective-permute-start.23 = (f32[512,128]{1,0:T(8,128)S(1)}, f32[512,128]{1,0:T(8,128)S(1)}, u32[]{:S(2)}, u32[]{:S(2)}) collective-permute-start(f32[512,128]{1,0:T(8,128)S(1)} %add_select_fusion), channel_id=1, source_target_pairs={{0,14},{2,0},{4,2},{6,4},{8,6},{10,8},{12,10},{14,12},{1,15},{3,1}... | collective-permute-start | bytes 786440 | tf_op jit(solution)/shard_map/ppermute | solution.py:275
  83.2 8.4 %collective-permute-start.22 = (f32[512,128]{1,0:T(8,128)S(1)}, f32[512,128]{1,0:T(8,128)S(1)}, u32[]{:S(2)}, u32[]{:S(2)}) collective-permute-start(f32[512,128]{1,0:T(8,128)S(1)} %add_select_fusion), channel_id=1, source_target_pairs={{0,2},{2,4},{4,6},{6,8},{8,10},{10,12},{12,14},{14,0},{1,3},{3,5},... | collective-permute-start | bytes 786440 | tf_op jit(solution)/shard_map/ppermute | solution.py:275
  84.7 7.0 %collective-permute-start.13 = (f32[384,128]{1,0:T(8,128)S(1)}, f32[384,128]{1,0:T(8,128)S(1)}, u32[]{:S(2)}, u32[]{:S(2)}) collective-permute-start(f32[384,128]{1,0:T(8,128)S(1)} %collective-permute-done.11), channel_id=1, source_target_pairs={{64,128},{65,129},{66,130},{67,131},{68,132},{69,133},{70,134},{71... | collective-permute-start | bytes 589832 | tf_op jit(solution)/shard_map/ppermute | solution.py:321
  90.2 6.2 %collective-permute-start.25 = (f32[512,128]{1,0:T(8,128)S(1)}, f32[512,128]{1,0:T(8,128)S(1)}, u32[]{:S(2)}, u32[]{:S(2)}) collective-permute-start(f32[512,128]{1,0:T(8,128)S(1)} %collective-permute-done.23), channel_id=1, source_target_pairs={{0,14},{2,0},{4,2},{6,4},{8,6},{10,8},{12,10},{14,12},{1,15},{3,1}... | collective-permute-start | bytes 786440 | tf_op jit(solution)/shard_map/ppermute | solution.py:275
  91.7 11.9 %collective-permute-start.24 = (f32[512,128]{1,0:T(8,128)S(1)}, f32[512,128]{1,0:T(8,128)S(1)}, u32[]{:S(2)}, u32[]{:S(2)}) collective-permute-start(f32[512,128]{1,0:T(8,128)S(1)} %collective-permute-done.22), channel_id=1, source_target_pairs={{0,2},{2,4},{4,6},{6,8},{8,10},{10,12},{12,14},{14,0},{1,3},{3,5},... | collective-permute-start | bytes 786440 | tf_op jit(solution)/shard_map/ppermute | solution.py:275
  91.7 8.9 %collective-permute-start.15 = (f32[384,128]{1,0:T(8,128)S(1)}, f32[384,128]{1,0:T(8,128)S(1)}, u32[]{:S(2)}, u32[]{:S(2)}) collective-permute-start(f32[384,128]{1,0:T(8,128)S(1)} %select_select_fusion), channel_id=1, source_target_pairs={{0,14},{2,0},{4,2},{6,4},{8,6},{10,8},{12,10},{14,12},{1,15},{3,1}... | collective-permute-start | bytes 589832 | tf_op jit(solution)/shard_map/ppermute | solution.py:275
  94.5 9.1 %collective-permute-start.14 = (f32[384,128]{1,0:T(8,128)S(1)}, f32[384,128]{1,0:T(8,128)S(1)}, u32[]{:S(2)}, u32[]{:S(2)}) collective-permute-start(f32[384,128]{1,0:T(8,128)S(1)} %select_select_fusion), channel_id=1, source_target_pairs={{0,2},{2,4},{4,6},{6,8},{8,10},{10,12},{12,14},{14,0},{1,3},{3,5},... | collective-permute-start | bytes 589832 | tf_op jit(solution)/shard_map/ppermute | solution.py:275
  96.4 11.9 %collective-permute-start.27 = (f32[512,128]{1,0:T(8,128)S(1)}, f32[512,128]{1,0:T(8,128)S(1)}, u32[]{:S(2)}, u32[]{:S(2)}) collective-permute-start(f32[512,128]{1,0:T(8,128)S(1)} %collective-permute-done.25), channel_id=1, source_target_pairs={{0,14},{2,0},{4,2},{6,4},{8,6},{10,8},{12,10},{14,12},{1,15},{3,1}... | collective-permute-start | bytes 786440 | tf_op jit(solution)/shard_map/ppermute | solution.py:275
  100.6 10.7 %collective-permute-start.17 = (f32[384,128]{1,0:T(8,128)S(1)}, f32[384,128]{1,0:T(8,128)S(1)}, u32[]{:S(2)}, u32[]{:S(2)}) collective-permute-start(f32[384,128]{1,0:T(8,128)S(1)} %collective-permute-done.15), channel_id=1, source_target_pairs={{0,14},{2,0},{4,2},{6,4},{8,6},{10,8},{12,10},{14,12},{1,15},{3,1}... | collective-permute-start | bytes 589832 | tf_op jit(solution)/shard_map/ppermute | solution.py:275
  103.6 9.4 %collective-permute-start.16 = (f32[384,128]{1,0:T(8,128)S(1)}, f32[384,128]{1,0:T(8,128)S(1)}, u32[]{:S(2)}, u32[]{:S(2)}) collective-permute-start(f32[384,128]{1,0:T(8,128)S(1)} %collective-permute-done.14), channel_id=1, source_target_pairs={{0,2},{2,4},{4,6},{6,8},{8,10},{10,12},{12,14},{14,0},{1,3},{3,5},... | collective-permute-start | bytes 589832 | tf_op jit(solution)/shard_map/ppermute | solution.py:275
  103.6 9.4 %collective-permute-start.26 = (f32[512,128]{1,0:T(8,128)S(1)}, f32[512,128]{1,0:T(8,128)S(1)}, u32[]{:S(2)}, u32[]{:S(2)}) collective-permute-start(f32[512,128]{1,0:T(8,128)S(1)} %collective-permute-done.24), channel_id=1, source_target_pairs={{0,2},{2,4},{4,6},{6,8},{8,10},{10,12},{12,14},{14,0},{1,3},{3,5},... | collective-permute-start | bytes 786440 | tf_op jit(solution)/shard_map/ppermute | solution.py:275
  103.7 43.5 %collective-permute-start.31 = (f32[1024,128]{1,0:T(8,128)S(1)}, f32[1024,128]{1,0:T(8,128)S(1)}, u32[]{:S(2)}, u32[]{:S(2)}) collective-permute-start(f32[1024,128]{1,0:T(8,128)S(1)} %pad_maximum_fusion), channel_id=1, source_target_pairs={{0,1},{1,0},{2,3},{3,2},{4,5},{5,4},{6,7},{7,6},{8,9},{9,8},{10,11... | collective-permute-start | bytes 1572872 | tf_op jit(solution)/shard_map/ppermute | solution.py:292
  108.3 9.9 %collective-permute-start.29 = (f32[256,128]{1,0:T(8,128)S(1)}, f32[256,128]{1,0:T(8,128)S(1)}, u32[]{:S(2)}, u32[]{:S(2)}) collective-permute-start(f32[256,128]{1,0:T(8,128)S(1)} %slice.30), channel_id=1, source_target_pairs={{0,14},{2,0},{4,2},{6,4},{8,6},{10,8},{12,10},{14,12},{1,15},{3,1}... | collective-permute-start | bytes 393224 | tf_op jit(solution)/shard_map/ppermute | solution.py:275
  111.3 7.0 %collective-permute-start.19 = (f32[384,128]{1,0:T(8,128)S(1)}, f32[384,128]{1,0:T(8,128)S(1)}, u32[]{:S(2)}, u32[]{:S(2)}) collective-permute-start(f32[384,128]{1,0:T(8,128)S(1)} %collective-permute-done.17), channel_id=1, source_target_pairs={{0,14},{2,0},{4,2},{6,4},{8,6},{10,8},{12,10},{14,12},{1,15},{3,1}... | collective-permute-start | bytes 589832 | tf_op jit(solution)/shard_map/ppermute | solution.py:275
  113.0 6.6 %collective-permute-start.18 = (f32[384,128]{1,0:T(8,128)S(1)}, f32[384,128]{1,0:T(8,128)S(1)}, u32[]{:S(2)}, u32[]{:S(2)}) collective-permute-start(f32[384,128]{1,0:T(8,128)S(1)} %collective-permute-done.16), channel_id=1, source_target_pairs={{0,2},{2,4},{4,6},{6,8},{8,10},{10,12},{12,14},{14,0},{1,3},{3,5},... | collective-permute-start | bytes 589832 | tf_op jit(solution)/shard_map/ppermute | solution.py:275
  113.0 34.2 %collective-permute-start.32 = (f32[1024,128]{1,0:T(8,128)S(1)}, f32[1024,128]{1,0:T(8,128)S(1)}, u32[]{:S(2)}, u32[]{:S(2)}) collective-permute-start(f32[1024,128]{1,0:T(8,128)S(1)} %pad_maximum_fusion.1), channel_id=1, source_target_pairs={{0,1},{1,0},{2,3},{3,2},{4,5},{5,4},{6,7},{7,6},{8,9},{9,8},{10,11... | collective-permute-start | bytes 1572872 | tf_op jit(solution)/shard_map/ppermute | solution.py:292
  118.2 29.7 %collective-permute-start.33 = (f32[1024,128]{1,0:T(8,128)S(1)}, f32[1024,128]{1,0:T(8,128)S(1)}, u32[]{:S(2)}, u32[]{:S(2)}) collective-permute-start(f32[1024,128]{1,0:T(8,128)S(1)} %pad_maximum_fusion.2), channel_id=1, source_target_pairs={{0,1},{1,0},{2,3},{3,2},{4,5},{5,4},{6,7},{7,6},{8,9},{9,8},{10,11... | collective-permute-start | bytes 1572872 | tf_op jit(solution)/shard_map/ppermute | solution.py:292
  118.4 5.6 %collective-permute-start.28 = (f32[256,128]{1,0:T(8,128)S(1)}, f32[256,128]{1,0:T(8,128)S(1)}, u32[]{:S(2)}, u32[]{:S(2)}) collective-permute-start(f32[256,128]{1,0:T(8,128)S(1)} %slice.29), channel_id=1, source_target_pairs={{0,2},{2,4},{4,6},{6,8},{8,10},{10,12},{12,14},{14,0},{1,3},{3,5},... | collective-permute-start | bytes 393224 | tf_op jit(solution)/shard_map/ppermute | solution.py:275
  119.6 6.7 %collective-permute-start.21 = (f32[192,128]{1,0:T(8,128)S(1)}, f32[192,128]{1,0:T(8,128)S(1)}, u32[]{:S(2)}, u32[]{:S(2)}) collective-permute-start(f32[192,128]{1,0:T(8,128)S(1)} %slice.28), channel_id=1, source_target_pairs={{0,14},{2,0},{4,2},{6,4},{8,6},{10,8},{12,10},{14,12},{1,15},{3,1}... | collective-permute-start | bytes 294920 | tf_op jit(solution)/shard_map/ppermute | solution.py:275
  123.9 23.2 %collective-permute-start.30 = (f32[512,128]{1,0:T(8,128)S(1)}, f32[512,128]{1,0:T(8,128)S(1)}, u32[]{:S(2)}, u32[]{:S(2)}) collective-permute-start(f32[512,128]{1,0:T(8,128)S(1)} %add_select_fusion), channel_id=1, source_target_pairs={{0,1},{1,0},{2,3},{3,2},{4,5},{5,4},{6,7},{7,6},{8,9},{9,8},{10,11... | collective-permute-start | bytes 786440 | tf_op jit(solution)/shard_map/ppermute | solution.py:292
  126.2 5.1 %collective-permute-start.20 = (f32[192,128]{1,0:T(8,128)S(1)}, f32[192,128]{1,0:T(8,128)S(1)}, u32[]{:S(2)}, u32[]{:S(2)}) collective-permute-start(f32[192,128]{1,0:T(8,128)S(1)} %slice.27), channel_id=1, source_target_pairs={{0,2},{2,4},{4,6},{6,8},{8,10},{10,12},{12,14},{14,0},{1,3},{3,5},... | collective-permute-start | bytes 294920 | tf_op jit(solution)/shard_map/ppermute | solution.py:275
  131.3 15.9 %collective-permute-start.34 = (f32[512,128]{1,0:T(8,128)S(1)}, f32[512,128]{1,0:T(8,128)S(1)}, u32[]{:S(2)}, u32[]{:S(2)}) collective-permute-start(f32[512,128]{1,0:T(8,128)S(1)} %pad_maximum_fusion.3), channel_id=1, source_target_pairs={{0,1},{1,0},{2,3},{3,2},{4,5},{5,4},{6,7},{7,6},{8,9},{9,8},{10,11... | collective-permute-start | bytes 786440 | tf_op jit(solution)/shard_map/ppermute | solution.py:292
  147.2 0.7 copy-start.4
  147.9 0.8 copy-start.2
  148.7 1.0 copy-start.3
  149.8 0.9 copy-start.5
Sparse Core Ops, SparseCore 0:
  83.3 51.2 all-gather.2
where the time goes:
time: 175 us; the launch traced here: 174 us
  waiting for transfers between devices  63.8 us (36%)
  starting transfers between devices  55.5 us (32%)
  Pallas kernels  32.3 us (18%)
  between operations  13.8 us (8%)
  local copies, waits for them, and re-layouts  8.59 us (5%)
    ppermute x1, waiting for transfers between devices, device(): lax.ppermute(mine, ROW + COL, [(r * 16 + j, j * 16 + r) for r in range(16...  32.1 us
    ppermute x16, starting transfers between devices, shift(): lax.ppermute(value, axis, [(i, (i + by) % size) for i in range(size)])  18.2 us
    pallas_call x1, Pallas kernels, main_math(): pl.pallas_call(main_kernel, grid=(4,), in_specs=[pl.BlockSpec(memory_spac...  16.9 us
    ppermute x16, waiting for transfers between devices, shift(): lax.ppermute(value, axis, [(i, (i + by) % size) for i in range(size)])  16.8 us
    ppermute x7, starting transfers between devices, device(): got = [lax.ppermute(pieces[k], 'z', [(0, k)]) for k in order]  15.6 us
    ppermute x5, starting transfers between devices, crossed(): return lax.ppermute(jnp.concatenate(values, 0), 'core', [(0, 1), (1, 0)])  14.1 us
    ppermute x7, waiting for transfers between devices, device(): got = [lax.ppermute(pieces[k], 'z', [(0, k)]) for k in order]  13.9 us
    pallas_call x1, Pallas kernels, head_math(): pl.pallas_call(head_kernel, in_specs=[pl.BlockSpec(memory_space=pltpu.SME...  13.8 us
  transfers between devices with their start and end apart: 36, of which 11 were waited for; matrix products, arithmetic and copies ran while one was open for 0% of the time, Pallas kernels for 8%

commit v1 on v0

--- a/solution.py
+++ b/solution.py
@@ -91,19 +91,15 @@
     return lax.fori_loop(1, 8, double, tuple(first))
 
 
-def head_kernel(place, *rest):
-    parts, (out, head, done, sems) = rest[:9], rest[9:]
-    z = place[2]
-    for offset, part in zip((0, -1, 1, -2, 2, -3, 3), parts):
-        head[(z + offset + SLABS) % SLABS] = part[...]
-    far = (z + 4) % SLABS
-    head[far, :6] = parts[7][...]
-    head[far, 6:] = parts[8][...]
+def head_kernel(parts, out, head, done, sems):
+    load = pltpu.make_async_copy(parts, head, sems.at[6])
+    load.start()
+    load.wait()
     rows, cols = iotas()
     eye = rows == cols
 
     def tile(k):
-        return jnp.concatenate([head[:, 2 * k + half].reshape(NB, 128) for half in range(2)], axis=1)
+        return jnp.concatenate([head[:, k // 3, 2 * (k % 3) + half].reshape(NB, 128) for half in range(2)], axis=1)
 
     a00, l00, a10, low, a11, l11 = (tile(k) for k in range(6))
     inv0, inv1 = inverses((l00, l11), rows, cols)
@@ -122,31 +118,29 @@
         copy.wait()
 
 
-def head_math(place, parts):
-    parts = [part.reshape(-1, SLAB, 128) for part in parts]
+def head_math(parts):
+    shape = (SLABS, 2, 6, SLAB, 128)
     return pl.pallas_call(
         head_kernel,
-        in_specs=[pl.BlockSpec(memory_space=pltpu.SMEM)] + [pl.BlockSpec(memory_space=pltpu.VMEM)] * 9,
+        in_specs=[pl.BlockSpec(memory_space=pltpu.HBM)],
         out_specs=pl.BlockSpec(memory_space=pltpu.HBM),
         out_shape=pltpu.HBM((6, NB, NB), jnp.float32),
         scratch_shapes=[
-            pltpu.VMEM((SLABS, 12, SLAB, 128), jnp.float32),
+            pltpu.VMEM(shape, jnp.float32),
             pltpu.VMEM((6, NB, NB), jnp.float32),
-            pltpu.SemaphoreType.DMA((6,)),
+            pltpu.SemaphoreType.DMA((7,)),
         ],
         compiler_params=pltpu.CompilerParams(vmem_limit_bytes=16 * 2**20),
         name="head",
-    )(place, *parts)
+    )(far(parts.reshape(shape)))
 
 
 def main_kernel(place, raw_far, local_far, head_far, *rest):
-    rows_in, rest = rest[:14], rest[14:]
+    grids, rest = rest[:10], rest[10:]
     out, raw_row, raw_col, local, head, col_hi, col_lo, head_hi, head_lo, sems = rest
     step = pl.program_id(0)
     p = place[0]
     c = place[1]
-    z = place[2]
-    core = c % 2
 
     def load_local(tile):
         return pltpu.make_async_copy(local_far.at[pl.ds(tile * 2048, 2048)], local.at[tile], sems.at[tile])
@@ -171,24 +165,29 @@
 
     @pl.when(step == 0)
     def _():
-        load_col = pltpu.make_async_copy(raw_far, raw_col, sems.at[4])
+        load_row = pltpu.make_async_copy(raw_far, raw_row, sems.at[4])
         load_head = pltpu.make_async_copy(head_far, head, sems.at[5])
         load_head.start()
-        load_col.start()
+        load_row.start()
         for tile in range(4):
             load_local(tile).start()
-        for which, side in ((0, core), (1, 1 - core)):
-            for k, offset in enumerate((0, -1, 1, -2, 2, -3, 3)):
-                part = rows_in[k] if which == 0 else rows_in[9 + (k + 1) // 2]
-                at = 0 if which == 0 or k == 0 else (k + 1) % 2
-                raw_row[(z + offset + SLABS) % SLABS, side] = part[at]
-            far = (z + 4) % SLABS
-            for m in range(2):
-                raw_row[far, side, m] = rows_in[7 + m][0] if which == 0 else rows_in[13][m]
+        y, x = p // 4, p % 4
+
+        def spot(dy, dx):
+            return (((y + dy) % 4) * 4 + (x + dx) % 4 + 16 - c) % 16
+
+        for m in range(2):
+            near, back, ahead, far_one, far_two = grids[5 * m : 5 * m + 5]
+            order = (0, 3, 1, 2)
+            for k in range(4):
+                for part, dy in ((near, 0), (back, 3), (ahead, 1), (far_one if k < 2 else far_two, 2)):
+                    dx = order[k]
+                    at = spot(dy, dx) if m == 0 else spot(dx, dy)
+                    index = k % 2 if dy == 2 else k
+                    raw_col[at // 2, at % 2, m] = part[index]
         load_head.wait()
         for k in range(6):
             head_hi[k], head_lo[k] = split(head[k])
-        load_col.wait()
 
         def one(tile, carry):
             g0, f0, g1, f1, _, _ = panels(raw_col, tile)
@@ -198,6 +197,7 @@
             return carry
 
         lax.fori_loop(0, 4, one, 0)
+        load_row.wait()
 
     g0, f0, g1, f1, done0, done1 = panels(raw_row, step)
     load_local(step).wait()
@@ -242,17 +242,15 @@
             put(0, jnp.where(rows >= cols, head[2 * block + 1], 0.0))
 
 
-def main_math(place, rows, raw_col, head, local):
+def main_math(place, raw_row, grids, head, local):
     raw = (SLABS, 2, 2, 4, 2, SLAB, 128)
     vmem = pl.BlockSpec(memory_space=pltpu.VMEM)
     hbm = pl.BlockSpec(memory_space=pltpu.HBM)
-    whole = [rows[k].reshape(-1, 2, 4, 2, SLAB, 128) for k in (0, 1, 2, 3, 4, 5, 6)]
-    halves = [rows[k].reshape(1, 4, 2, SLAB, 128) for k in (7, 8)]
-    crossed = [rows[k].reshape(-1, 2, 4, 2, SLAB, 128) for k in (9, 10, 11, 12)] + [rows[13].reshape(2, 4, 2, SLAB, 128)]
+    grids = [part.reshape(-1, 4, 2, SLAB, 128) for part in grids]
     return pl.pallas_call(
         main_kernel,
         grid=(4,),
-        in_specs=[pl.BlockSpec(memory_space=pltpu.SMEM), hbm, hbm, hbm] + [vmem] * 14,
+        in_specs=[pl.BlockSpec(memory_space=pltpu.SMEM), hbm, hbm, hbm] + [vmem] * 10,
         out_specs=pl.BlockSpec((2048, 128), lambda i: (i, 0)),
         out_shape=jax.ShapeDtypeStruct((8192, 128), jnp.float32),
         scratch_shapes=[
@@ -268,28 +266,21 @@
         ],
         compiler_params=pltpu.CompilerParams(vmem_limit_bytes=32 * 2**20),
         name="main",
-    )(place, far(raw_col.reshape(raw)), far(local), far(head), *whole, *halves, *crossed)
+    )(place, far(raw_row.reshape(raw)), far(local), far(head), *grids)
 
 
 def shift(value, axis, size, by):
     return lax.ppermute(value, axis, [(i, (i + by) % size) for i in range(size)])
 
 
-def ring8(value):
-    up1, down1 = shift(value, "z", 8, 1), shift(value, "z", 8, -1)
-    up2, down2 = shift(up1, "z", 8, 1), shift(down1, "z", 8, -1)
-    up3, down3 = shift(up2, "z", 8, 1), shift(down2, "z", 8, -1)
-    half = value.shape[0] // 2
-    up4, down4 = shift(up3[:half], "z", 8, 1), shift(down3[half:], "z", 8, -1)
-    return [value, up1, down1, up2, down2, up3, down3, up4, down4]
-
-
 def far(value):
     return pltpu.with_memory_space_constraint(value, pltpu.HBM)
 
 
-def crossed(*values):
-    return lax.ppermute(jnp.concatenate(values, 0), "core", [(0, 1), (1, 0)])
+def ring4(value, axis):
+    up, down = shift(value, axis, 4, 1), shift(value, axis, 4, -1)
+    half = value.shape[0] // 2
+    return [value, up, down, shift(up[:half], axis, 4, 1), shift(down[half:], axis, 4, -1)]
 
 
 def device(matrix, factor):
@@ -305,7 +296,11 @@
     for value in got[1:]:
         total = total + value
     mine = jnp.where(z == 0, pieces[0], total)
-    swapped = lax.ppermute(mine, ROW + COL, [(r * 16 + j, j * 16 + r) for r in range(16) for j in range(16)])
+    raw_row = lax.all_gather(mine, COL)
+
+    moved = lax.ppermute(mine, ROW + COL, [(r * 16 + j, (j + r) % 16 * 16 + j) for r in range(16) for j in range(16)])
+    swapped = lax.ppermute(moved, ROW + COL, [(q * 16 + j, q * 16 + (q - j) % 16) for q in range(16) for j in range(16)])
+
     top = mine.reshape(2, 4, 2 * SLAB, 128)[:, 0].reshape(4 * SLAB, 128)
     other = lax.ppermute(top, "core", [(0, 1), (1, 0)])
     both = jnp.where(core == 0, jnp.concatenate([top, other], 0), jnp.concatenate([other, top], 0))
@@ -316,14 +311,16 @@
     head = jnp.where(x < 2, head, sent)
     sent1 = lax.ppermute(head, "y", [(0, 1)])
     sent3 = lax.ppermute(head, "y", [(0, 3)])
-    swapped, sent1, sent3 = lax.optimization_barrier((swapped, sent1, sent3))
-    raw_col = lax.all_gather(swapped, ROW)
     sent2 = lax.ppermute(sent1, "y", [(1, 2)])
     head = jnp.where(y == 0, head, jnp.where(y == 1, sent1, jnp.where(y == 2, sent2, sent3)))
-    head = head_math(place, ring8(head))
-    rows = ring8(mine)
-    rows = rows + [crossed(*rows[k : k + 2]) if k else crossed(rows[0]) for k in (0, 1, 3, 5, 7)]
-    return main_math(place, rows, raw_col, head, local).reshape(matrix.shape)
+    half = jnp.where(core == 0, head[: 6 * SLAB], head[6 * SLAB :])
+    half = lax.all_gather(half, COL)
+    head = head_math(half)
+
+    first = ring4(swapped[: 8 * SLAB], "x")
+    second = ring4(swapped[8 * SLAB :], "y")
+    grids = ring4(jnp.concatenate(first, 0), "y") + ring4(jnp.concatenate(second, 0), "x")
+    return main_math(place, raw_row, grids, head, local).reshape(matrix.shape)
 
 
 def solution(mesh):

time: 175 us -> 179 us (1.023)
  the two profiles are of different devices: /device:TPU:31 before, /device:TPU:2 now
where the time goes in v1:
time: 179 us; the launch traced here: 177 us
  starting transfers between devices  72.7 us (41%)
  waiting for transfers between devices  49.3 us (28%)
  Pallas kernels  33 us (18%)
  between operations  13.8 us (8%)
  local copies, waits for them, and re-layouts  7.43 us (4%)
    ppermute x16, starting transfers between devices, shift(): lax.ppermute(value, axis, [(i, (i + by) % size) for i in range(size)])  42 us
    pallas_call x1, Pallas kernels, main_math(): pl.pallas_call(main_kernel, grid=(4,), in_specs=[pl.BlockSpec(memory_spac...  16.8 us
    ppermute x7, starting transfers between devices, device(): got = [lax.ppermute(pieces[k], 'z', [(0, k)]) for k in order]  15.9 us
    pallas_call x1, Pallas kernels, head_math(): pl.pallas_call(head_kernel, in_specs=[pl.BlockSpec(memory_space=pltpu.HBM...  14.6 us
    ppermute x7, waiting for transfers between devices, device(): got = [lax.ppermute(pieces[k], 'z', [(0, k)]) for k in order]  14.5 us
    all_gather x1, waiting for transfers between devices, device(): raw_row = lax.all_gather(mine, COL)  10.6 us
    ppermute x16, waiting for transfers between devices, shift(): lax.ppermute(value, axis, [(i, (i + by) % size) for i in range(size)])  9.66 us
    ppermute x1, starting transfers between devices, device(): lax.ppermute(moved, ROW + COL, [(q * 16 + j, q * 16 + (q - j) % 16) for q...  6.02 us
  transfers between devices with their start and end apart: 33, of which 14 were waited for; matrix products, arithmetic and copies ran while one was open for 2% of the time, Pallas kernels for 8%

profile of v1, /device:TPU:2, one launch (start us, length us, event | category | flops | bytes accessed | tf_op | source)
XLA Modules:
  0.0 177.2 jit_solution(11876498337977689692)
XLA Ops:
  6.5 0.1 pad_add_fusion.place
  6.6 2.2 %copy-done = f32[4,1,256,4,1,256]{5,4,3,2,1,0:T(1,128)S(1)} copy-done((f32[4,1,256,4,1,256]{5,4,3,2,1,0:T(1,128)S(1)}, f32[4,1,256,4,1,256]{5,4,3,2,1,0:T(1,128)}, u32[]{:S(2)}) %copy-start) | copy-done | bytes 4194328
  8.8 2.2 %copy-done.1 = f32[4,1,256,4,1,256]{5,4,3,2,1,0:T(1,128)S(1)} copy-done((f32[4,1,256,4,1,256]{5,4,3,2,1,0:T(1,128)S(1)}, f32[4,1,256,4,1,256]{5,4,3,2,1,0:T(1,128)}, u32[]{:S(2)}) %copy-start.1) | copy-done | bytes 4194328
  11.0 1.7 pack.1
  12.7 8.1 %collective-permute-start = (f32[512,128]{1,0:T(8,128)S(1)}, f32[512,128]{1,0:T(8,128)S(1)}, u32[]{:S(2)}, u32[]{:S(2)}) collective-permute-start(f32[512,128]{1,0:T(8,128)S(1)} %get-tuple-element.14), channel_id=1, source_target_pairs={{0,8},{1,9},{16,24},{17,25},{32,40},{33,41},{48,56},{49,57},{64,72... | collective-permute-start | bytes 786440 | tf_op jit(solution)/shard_map/ppermute | solution.py:294
  20.7 1.3 collective-permute-start.1
  22.0 1.3 collective-permute-start.2
  23.4 1.3 collective-permute-start.3
  24.7 1.3 collective-permute-start.4
  26.0 1.4 collective-permute-done
  27.4 1.3 collective-permute-start.5
  28.7 4.3 %collective-permute-done.1 = f32[512,128]{1,0:T(8,128)S(1)} collective-permute-done((f32[512,128]{1,0:T(8,128)S(1)}, f32[512,128]{1,0:T(8,128)S(1)}, u32[]{:S(2)}, u32[]{:S(2)}) %collective-permute-start.1) | collective-permute-done | bytes 262176 | tf_op jit(solution)/shard_map/ppermute | solution.py:294
  33.0 1.3 collective-permute-start.6
  34.3 4.3 %collective-permute-done.3 = f32[512,128]{1,0:T(8,128)S(1)} collective-permute-done((f32[512,128]{1,0:T(8,128)S(1)}, f32[512,128]{1,0:T(8,128)S(1)}, u32[]{:S(2)}, u32[]{:S(2)}) %collective-permute-start.3) | collective-permute-done | bytes 262176 | tf_op jit(solution)/shard_map/ppermute | solution.py:294
  38.6 4.5 %collective-permute-done.5 = f32[512,128]{1,0:T(8,128)S(1)} collective-permute-done((f32[512,128]{1,0:T(8,128)S(1)}, f32[512,128]{1,0:T(8,128)S(1)}, u32[]{:S(2)}, u32[]{:S(2)}) %collective-permute-start.5) | collective-permute-done | bytes 262176 | tf_op jit(solution)/shard_map/ppermute | solution.py:294
  43.1 0.0 collective-permute-done.6
  43.1 0.1 add_select_fusion
  43.2 0.0 copy-start.2
  43.2 0.1 collective-permute-start.7
  43.4 1.2 collective-permute-done.7
  44.6 2.4 %collective-permute-start.8 = (f32[256,128]{1,0:T(8,128)S(1)}, f32[256,128]{1,0:T(8,128)S(1)}, u32[]{:S(2)}, u32[]{:S(2)}) collective-permute-start(f32[256,128]{1,0:T(8,128)S(1)} %maximum_select_fusion), channel_id=1, source_target_pairs={{0,16},{16,0},{1,17},{17,1},{2,18},{18,2},{3,19},{19,3},{4,20},{20... | collective-permute-start | bytes 393224 | tf_op jit(solution)/shard_map/ppermute | solution.py:307
  47.1 5.0 %collective-permute-done.8 = f32[256,128]{1,0:T(8,128)S(1)} collective-permute-done((f32[256,128]{1,0:T(8,128)S(1)}, f32[256,128]{1,0:T(8,128)S(1)}, u32[]{:S(2)}, u32[]{:S(2)}) %collective-permute-start.8) | collective-permute-done | bytes 131104 | tf_op jit(solution)/shard_map/ppermute | solution.py:307
  52.1 1.3 collective-permute-start.9
  53.4 3.9 %collective-permute-done.9 = f32[384,128]{1,0:T(8,128)S(1)} collective-permute-done((f32[384,128]{1,0:T(8,128)S(1)}, f32[384,128]{1,0:T(8,128)S(1)}, u32[]{:S(2)}, u32[]{:S(2)}) %collective-permute-start.9) | collective-permute-done | bytes 196640 | tf_op jit(solution)/shard_map/ppermute | solution.py:310
  57.3 1.3 collective-permute-start.10
  58.6 1.3 collective-permute-start.12
  59.9 2.0 %collective-permute-done.10 = f32[384,128]{1,0:T(8,128)S(1)} collective-permute-done((f32[384,128]{1,0:T(8,128)S(1)}, f32[384,128]{1,0:T(8,128)S(1)}, u32[]{:S(2)}, u32[]{:S(2)}) %collective-permute-start.10) | collective-permute-done | bytes 196640 | tf_op jit(solution)/shard_map/ppermute | solution.py:312
  61.9 0.7 collective-permute-start.11
  62.6 0.6 collective-permute-done.12
  63.3 0.7 slice_select_fusion
  63.9 0.0 all-gather.7.cloned.1.call-update
  64.0 0.0 all-gather.5.cloned.1.call-start
  64.0 0.7 all-gather.5.cloned.1.call-update
  64.7 1.6 collective-permute-start.13
  66.3 0.0 collective-permute-done.13
  66.3 6.0 %collective-permute-start.14 = (f32[512,128]{1,0:T(8,128)S(1)}, f32[512,128]{1,0:T(8,128)S(1)}, u32[]{:S(2)}, u32[]{:S(2)}) collective-permute-start(f32[512,128]{1,0:T(8,128)S(1)} %collective-permute-done.13), channel_id=1, source_target_pairs={{0,0},{1,15},{2,14},{3,13},{4,12},{5,11},{6,10},{7,9},{8,8},{9,7},... | collective-permute-start | bytes 786440 | tf_op jit(solution)/shard_map/ppermute | solution.py:302
  72.4 1.1 collective-permute-done.14
  73.5 8.3 %collective-permute-start.24 = (f32[256,128]{1,0:T(8,128)S(1)}, f32[256,128]{1,0:T(8,128)S(1)}, u32[]{:S(2)}, u32[]{:S(2)}) collective-permute-start(f32[256,128]{1,0:T(8,128)S(1)} %get-tuple-element.21), channel_id=1, source_target_pairs={{0,192},{64,0},{128,64},{192,128},{1,193},{65,1},{129,65},{193,129... | collective-permute-start | bytes 393224 | tf_op jit(solution)/shard_map/ppermute | solution.py:273
  81.8 1.1 collective-permute-start.23
  82.9 8.3 %collective-permute-start.16 = (f32[256,128]{1,0:T(8,128)S(1)}, f32[256,128]{1,0:T(8,128)S(1)}, u32[]{:S(2)}, u32[]{:S(2)}) collective-permute-start(f32[256,128]{1,0:T(8,128)S(1)} %get-tuple-element.24), channel_id=1, source_target_pairs={{0,48},{16,0},{32,16},{48,32},{1,49},{17,1},{33,17},{49,33},{2,50}... | collective-permute-start | bytes 393224 | tf_op jit(solution)/shard_map/ppermute | solution.py:273
  91.2 4.5 %collective-permute-start.15 = (f32[256,128]{1,0:T(8,128)S(1)}, f32[256,128]{1,0:T(8,128)S(1)}, u32[]{:S(2)}, u32[]{:S(2)}) collective-permute-start(f32[256,128]{1,0:T(8,128)S(1)} %get-tuple-element.24), channel_id=1, source_target_pairs={{0,16},{16,32},{32,48},{48,0},{1,17},{17,33},{33,49},{49,1},{2,18}... | collective-permute-start | bytes 393224 | tf_op jit(solution)/shard_map/ppermute | solution.py:273
  95.8 3.7 %collective-permute-start.26 = (f32[128,128]{1,0:T(8,128)S(1)}, f32[128,128]{1,0:T(8,128)S(1)}, u32[]{:S(2)}, u32[]{:S(2)}) collective-permute-start(f32[128,128]{1,0:T(8,128)S(1)} %slice.68), channel_id=1, source_target_pairs={{0,192},{64,0},{128,64},{192,128},{1,193},{65,1},{129,65},{193,129... | collective-permute-start | bytes 196616 | tf_op jit(solution)/shard_map/ppermute | solution.py:273
  99.5 0.1 collective-permute-start.25
  99.6 0.0 collective-permute-done.16
  99.6 0.1 collective-permute-start.18
  99.7 3.2 %collective-permute-start.17 = (f32[128,128]{1,0:T(8,128)S(1)}, f32[128,128]{1,0:T(8,128)S(1)}, u32[]{:S(2)}, u32[]{:S(2)}) collective-permute-start(f32[128,128]{1,0:T(8,128)S(1)} %slice.62), channel_id=1, source_target_pairs={{0,16},{16,32},{32,48},{48,0},{1,17},{17,33},{33,49},{49,1},{2,18}... | collective-permute-start | bytes 196616 | tf_op jit(solution)/shard_map/ppermute | solution.py:273
  103.0 1.8 %collective-permute-done.17 = f32[128,128]{1,0:T(8,128)S(1)} collective-permute-done((f32[128,128]{1,0:T(8,128)S(1)}, f32[128,128]{1,0:T(8,128)S(1)}, u32[]{:S(2)}, u32[]{:S(2)}) %collective-permute-start.17) | collective-permute-done | bytes 65568 | tf_op jit(solution)/shard_map/ppermute | solution.py:273
  104.8 0.2 collective-permute-done.18
  105.0 3.4 %collective-permute-start.20 = (f32[1024,128]{1,0:T(8,128)S(1)}, f32[1024,128]{1,0:T(8,128)S(1)}, u32[]{:S(2)}, u32[]{:S(2)}) collective-permute-start(f32[1024,128]{1,0:T(8,128)S(1)} %constant_dynamic-update-slice_fusion), channel_id=1, source_target_pairs={{0,192},{64,0},{128,64},{192,128},{1,193},{65,1},{129,65},{193,129... | collective-permute-start | bytes 1572872 | tf_op jit(solution)/shard_map/ppermute | solution.py:273
  108.4 0.0 collective-permute-start.19
  108.4 0.0 collective-permute-done.25
  108.5 3.3 %collective-permute-start.28 = (f32[1024,128]{1,0:T(8,128)S(1)}, f32[1024,128]{1,0:T(8,128)S(1)}, u32[]{:S(2)}, u32[]{:S(2)}) collective-permute-start(f32[1024,128]{1,0:T(8,128)S(1)} %constant_dynamic-update-slice_fusion.5), channel_id=1, source_target_pairs={{0,48},{16,0},{32,16},{48,32},{1,49},{17,1},{33,17},{49,33},{2,50}... | collective-permute-start | bytes 1572872 | tf_op jit(solution)/shard_map/ppermute | solution.py:273
  111.8 0.0 collective-permute-start.27
  111.8 7.6 %collective-permute-done.20 = f32[1024,128]{1,0:T(8,128)S(1)} collective-permute-done((f32[1024,128]{1,0:T(8,128)S(1)}, f32[1024,128]{1,0:T(8,128)S(1)}, u32[]{:S(2)}, u32[]{:S(2)}) %collective-permute-start.20) | collective-permute-done | bytes 524320 | tf_op jit(solution)/shard_map/ppermute | solution.py:273
  119.4 0.7 slice.65
  120.1 3.5 %collective-permute-start.22 = (f32[512,128]{1,0:T(8,128)}, f32[512,128]{1,0:T(8,128)S(1)}, u32[]{:S(2)}, u32[]{:S(2)}) collective-permute-start(f32[512,128]{1,0:T(8,128)} %slice.65), channel_id=1, source_target_pairs={{0,192},{64,0},{128,64},{192,128},{1,193},{65,1},{129,65},{193,129... | collective-permute-start | bytes 786440 | tf_op jit(solution)/shard_map/ppermute | solution.py:273
  123.6 0.7 slice.64
  124.3 0.7 slice.70
  125.0 2.6 %collective-permute-start.30 = (f32[512,128]{1,0:T(8,128)}, f32[512,128]{1,0:T(8,128)}, u32[]{:S(2)}, u32[]{:S(2)}) collective-permute-start(f32[512,128]{1,0:T(8,128)} %slice.70), channel_id=1, source_target_pairs={{0,48},{16,0},{32,16},{48,32},{1,49},{17,1},{33,17},{49,33},{2,50}... | collective-permute-start | bytes 786440 | tf_op jit(solution)/shard_map/ppermute | solution.py:273
  127.6 0.0 collective-permute-done.27
  127.6 0.7 slice.69
  128.3 14.6 %head.1.head_far = f32[6,256,256]{2,1,0:T(8,128)} custom-call(f32[8,2,6,32,128]{4,3,2,1,0:T(8,128)} %bitcast.31), custom_call_target="tpu_custom_call" | custom-call | tf_op jit(solution)/shard_map/head/pallas_call | solution.py:123
  143.0 10.6 %all-gather.5.cloned.1.call-done = f32[8192,128]{1,0:T(8,128)} async-done(((f32[512,128]{1,0:T(8,128)}), f32[8192,128]{1,0:T(8,128)}) %all-gather.5.cloned.1.call-update) | async-done | bytes 4194320 | tf_op jit(solution)/shard_map/all_gather | solution.py:299
  153.6 16.8 %main.1 = f32[8192,128]{1,0:T(8,128)} custom-call(s32[3]{0:T(128)S(1)} %pad_add_fusion.place, f32[8,2,2,4,2,32,128]{6,5,4,3,2,1,0:T(8,128)} %bitcast.30, f32[8192,128]{1,0:T(8,128)} %bitcast.20, f32[6,256,256]{2,1,0:T(8,128)} %head.1.head_far, f32[4,4,2,32,128]{4,3,2,1,0:T(8,128)S(1)} %bitcast.27, f32[4,4,2,32,128]{4,3,2,1,0:T(8,128)S(1)} %bitcast.24, ...), custom_call_target="tpu_custom_call" | custom-call | tf_op jit(solution)/shard_map/main/pallas_call | solution.py:250
  (40 shorter events, 0.3 us)
Async XLA Ops:
  6.5 121.8 %all-gather.7.cloned.1.call-start = ((), (), s32[]{:S(2)}) async-start(), calls=%async_computation.1 | async-start | bytes 1671168 | tf_op jit(solution)/shard_map/all_gather | solution.py:317
  6.6 2.2 %copy-start = (f32[4,1,256,4,1,256]{5,4,3,2,1,0:T(1,128)S(1)}, f32[4,1,256,4,1,256]{5,4,3,2,1,0:T(1,128)}, u32[]{:S(2)}) copy-start(f32[4,1,256,4,1,256]{5,4,3,2,1,0:T(1,128)} %param.2) | copy-start | bytes 12582916
  8.8 2.2 %copy-start.1 = (f32[4,1,256,4,1,256]{5,4,3,2,1,0:T(1,128)S(1)}, f32[4,1,256,4,1,256]{5,4,3,2,1,0:T(1,128)}, u32[]{:S(2)}) copy-start(f32[4,1,256,4,1,256]{5,4,3,2,1,0:T(1,128)} %param.3) | copy-start | bytes 12582916
  12.7 14.7 %collective-permute-start = (f32[512,128]{1,0:T(8,128)S(1)}, f32[512,128]{1,0:T(8,128)S(1)}, u32[]{:S(2)}, u32[]{:S(2)}) collective-permute-start(f32[512,128]{1,0:T(8,128)S(1)} %get-tuple-element.14), channel_id=1, source_target_pairs={{0,8},{1,9},{16,24},{17,25},{32,40},{33,41},{48,56},{49,57},{64,72... | collective-permute-start | bytes 786440 | tf_op jit(solution)/shard_map/ppermute | solution.py:294
  20.7 12.3 %collective-permute-start.1 = (f32[512,128]{1,0:T(8,128)S(1)}, f32[512,128]{1,0:T(8,128)S(1)}, u32[]{:S(2)}, u32[]{:S(2)}) collective-permute-start(f32[512,128]{1,0:T(8,128)S(1)} %get-tuple-element.15), channel_id=1, source_target_pairs={{0,2},{1,3},{16,18},{17,19},{32,34},{33,35},{48,50},{49,51},{64,66... | collective-permute-start | bytes 786440 | tf_op jit(solution)/shard_map/ppermute | solution.py:294
  22.0 12.3 %collective-permute-start.2 = (f32[512,128]{1,0:T(8,128)S(1)}, f32[512,128]{1,0:T(8,128)S(1)}, u32[]{:S(2)}, u32[]{:S(2)}) collective-permute-start(f32[512,128]{1,0:T(8,128)S(1)} %get-tuple-element.16), channel_id=1, source_target_pairs={{0,14},{1,15},{16,30},{17,31},{32,46},{33,47},{48,62},{49,63},{64,... | collective-permute-start | bytes 786440 | tf_op jit(solution)/shard_map/ppermute | solution.py:294
  23.4 15.3 %collective-permute-start.3 = (f32[512,128]{1,0:T(8,128)S(1)}, f32[512,128]{1,0:T(8,128)S(1)}, u32[]{:S(2)}, u32[]{:S(2)}) collective-permute-start(f32[512,128]{1,0:T(8,128)S(1)} %get-tuple-element.17), channel_id=1, source_target_pairs={{0,4},{1,5},{16,20},{17,21},{32,36},{33,37},{48,52},{49,53},{64,68... | collective-permute-start | bytes 786440 | tf_op jit(solution)/shard_map/ppermute | solution.py:294
  24.7 14.0 %collective-permute-start.4 = (f32[512,128]{1,0:T(8,128)S(1)}, f32[512,128]{1,0:T(8,128)S(1)}, u32[]{:S(2)}, u32[]{:S(2)}) collective-permute-start(f32[512,128]{1,0:T(8,128)S(1)} %get-tuple-element.18), channel_id=1, source_target_pairs={{0,12},{1,13},{16,28},{17,29},{32,44},{33,45},{48,60},{49,61},{64,... | collective-permute-start | bytes 786440 | tf_op jit(solution)/shard_map/ppermute | solution.py:294
  27.4 15.7 %collective-permute-start.5 = (f32[512,128]{1,0:T(8,128)S(1)}, f32[512,128]{1,0:T(8,128)S(1)}, u32[]{:S(2)}, u32[]{:S(2)}) collective-permute-start(f32[512,128]{1,0:T(8,128)S(1)} %get-tuple-element.19), channel_id=1, source_target_pairs={{0,6},{1,7},{16,22},{17,23},{32,38},{33,39},{48,54},{49,55},{64,70... | collective-permute-start | bytes 786440 | tf_op jit(solution)/shard_map/ppermute | solution.py:294
  33.0 10.1 %collective-permute-start.6 = (f32[512,128]{1,0:T(8,128)S(1)}, f32[512,128]{1,0:T(8,128)S(1)}, u32[]{:S(2)}, u32[]{:S(2)}) collective-permute-start(f32[512,128]{1,0:T(8,128)S(1)} %get-tuple-element.20), channel_id=1, source_target_pairs={{0,10},{1,11},{16,26},{17,27},{32,42},{33,43},{48,58},{49,59},{64,... | collective-permute-start | bytes 786440 | tf_op jit(solution)/shard_map/ppermute | solution.py:294
  43.2 20.8 %copy-start.2 = (f32[512,128]{1,0:T(8,128)}, f32[512,128]{1,0:T(8,128)S(1)}, u32[]{:S(2)}) copy-start(f32[512,128]{1,0:T(8,128)S(1)} %add_select_fusion) | copy-start | bytes 786436
  43.2 1.3 collective-permute-start.7
  44.6 7.5 %collective-permute-start.8 = (f32[256,128]{1,0:T(8,128)S(1)}, f32[256,128]{1,0:T(8,128)S(1)}, u32[]{:S(2)}, u32[]{:S(2)}) collective-permute-start(f32[256,128]{1,0:T(8,128)S(1)} %maximum_select_fusion), channel_id=1, source_target_pairs={{0,16},{16,0},{1,17},{17,1},{2,18},{18,2},{3,19},{19,3},{4,20},{20... | collective-permute-start | bytes 393224 | tf_op jit(solution)/shard_map/ppermute | solution.py:307
  52.1 5.2 %collective-permute-start.9 = (f32[384,128]{1,0:T(8,128)S(1)}, f32[384,128]{1,0:T(8,128)S(1)}, u32[]{:S(2)}, u32[]{:S(2)}) collective-permute-start(f32[384,128]{1,0:T(8,128)S(1)} %pad_maximum_fusion), channel_id=1, source_target_pairs={{0,48},{16,32},{1,49},{17,33},{2,50},{18,34},{3,51},{19,35},{4,52}... | collective-permute-start | bytes 589832 | tf_op jit(solution)/shard_map/ppermute | solution.py:310
  57.3 4.6 %collective-permute-start.10 = (f32[384,128]{1,0:T(8,128)S(1)}, f32[384,128]{1,0:T(8,128)S(1)}, u32[]{:S(2)}, u32[]{:S(2)}) collective-permute-start(f32[384,128]{1,0:T(8,128)S(1)} %broadcast_select_fusion), channel_id=1, source_target_pairs={{0,64},{1,65},{2,66},{3,67},{4,68},{5,69},{6,70},{7,71},{8,72},{9,... | collective-permute-start | bytes 589832 | tf_op jit(solution)/shard_map/ppermute | solution.py:312
  58.6 4.6 %collective-permute-start.12 = (f32[384,128]{1,0:T(8,128)S(1)}, f32[384,128]{1,0:T(8,128)S(1)}, u32[]{:S(2)}, u32[]{:S(2)}) collective-permute-start(f32[384,128]{1,0:T(8,128)S(1)} %broadcast_select_fusion), channel_id=1, source_target_pairs={{0,192},{1,193},{2,194},{3,195},{4,196},{5,197},{6,198},{7,199},{8... | collective-permute-start | bytes 589832 | tf_op jit(solution)/shard_map/ppermute | solution.py:313
  61.9 1.3 collective-permute-start.11
  64.0 89.6 %all-gather.5.cloned.1.call-start = ((), (), s32[]{:S(2)}) async-start(), calls=%async_computation | async-start | bytes 4456448 | tf_op jit(solution)/shard_map/all_gather | solution.py:299
  64.7 1.6 collective-permute-start.13
  66.3 7.2 %collective-permute-start.14 = (f32[512,128]{1,0:T(8,128)S(1)}, f32[512,128]{1,0:T(8,128)S(1)}, u32[]{:S(2)}, u32[]{:S(2)}) collective-permute-start(f32[512,128]{1,0:T(8,128)S(1)} %collective-permute-done.13), channel_id=1, source_target_pairs={{0,0},{1,15},{2,14},{3,13},{4,12},{5,11},{6,10},{7,9},{8,8},{9,7},... | collective-permute-start | bytes 786440 | tf_op jit(solution)/shard_map/ppermute | solution.py:302
  73.5 22.2 %collective-permute-start.24 = (f32[256,128]{1,0:T(8,128)S(1)}, f32[256,128]{1,0:T(8,128)S(1)}, u32[]{:S(2)}, u32[]{:S(2)}) collective-permute-start(f32[256,128]{1,0:T(8,128)S(1)} %get-tuple-element.21), channel_id=1, source_target_pairs={{0,192},{64,0},{128,64},{192,128},{1,193},{65,1},{129,65},{193,129... | collective-permute-start | bytes 393224 | tf_op jit(solution)/shard_map/ppermute | solution.py:273
  81.8 17.7 %collective-permute-start.23 = (f32[256,128]{1,0:T(8,128)S(1)}, f32[256,128]{1,0:T(8,128)S(1)}, u32[]{:S(2)}, u32[]{:S(2)}) collective-permute-start(f32[256,128]{1,0:T(8,128)S(1)} %get-tuple-element.21), channel_id=1, source_target_pairs={{0,64},{64,128},{128,192},{192,0},{1,65},{65,129},{129,193},{193,1... | collective-permute-start | bytes 393224 | tf_op jit(solution)/shard_map/ppermute | solution.py:273
  82.9 16.7 %collective-permute-start.16 = (f32[256,128]{1,0:T(8,128)S(1)}, f32[256,128]{1,0:T(8,128)S(1)}, u32[]{:S(2)}, u32[]{:S(2)}) collective-permute-start(f32[256,128]{1,0:T(8,128)S(1)} %get-tuple-element.24), channel_id=1, source_target_pairs={{0,48},{16,0},{32,16},{48,32},{1,49},{17,1},{33,17},{49,33},{2,50}... | collective-permute-start | bytes 393224 | tf_op jit(solution)/shard_map/ppermute | solution.py:273
  91.2 8.5 %collective-permute-start.15 = (f32[256,128]{1,0:T(8,128)S(1)}, f32[256,128]{1,0:T(8,128)S(1)}, u32[]{:S(2)}, u32[]{:S(2)}) collective-permute-start(f32[256,128]{1,0:T(8,128)S(1)} %get-tuple-element.24), channel_id=1, source_target_pairs={{0,16},{16,32},{32,48},{48,0},{1,17},{17,33},{33,49},{49,1},{2,18}... | collective-permute-start | bytes 393224 | tf_op jit(solution)/shard_map/ppermute | solution.py:273
  95.8 12.7 %collective-permute-start.26 = (f32[128,128]{1,0:T(8,128)S(1)}, f32[128,128]{1,0:T(8,128)S(1)}, u32[]{:S(2)}, u32[]{:S(2)}) collective-permute-start(f32[128,128]{1,0:T(8,128)S(1)} %slice.68), channel_id=1, source_target_pairs={{0,192},{64,0},{128,64},{192,128},{1,193},{65,1},{129,65},{193,129... | collective-permute-start | bytes 196616 | tf_op jit(solution)/shard_map/ppermute | solution.py:273
  99.5 9.0 %collective-permute-start.25 = (f32[128,128]{1,0:T(8,128)S(1)}, f32[128,128]{1,0:T(8,128)S(1)}, u32[]{:S(2)}, u32[]{:S(2)}) collective-permute-start(f32[128,128]{1,0:T(8,128)S(1)} %slice.67), channel_id=1, source_target_pairs={{0,64},{64,128},{128,192},{192,0},{1,65},{65,129},{129,193},{193,1... | collective-permute-start | bytes 196616 | tf_op jit(solution)/shard_map/ppermute | solution.py:273
  99.6 5.4 %collective-permute-start.18 = (f32[128,128]{1,0:T(8,128)S(1)}, f32[128,128]{1,0:T(8,128)S(1)}, u32[]{:S(2)}, u32[]{:S(2)}) collective-permute-start(f32[128,128]{1,0:T(8,128)S(1)} %slice.63), channel_id=1, source_target_pairs={{0,48},{16,0},{32,16},{48,32},{1,49},{17,1},{33,17},{49,33},{2,50}... | collective-permute-start | bytes 196616 | tf_op jit(solution)/shard_map/ppermute | solution.py:273
  99.7 5.1 %collective-permute-start.17 = (f32[128,128]{1,0:T(8,128)S(1)}, f32[128,128]{1,0:T(8,128)S(1)}, u32[]{:S(2)}, u32[]{:S(2)}) collective-permute-start(f32[128,128]{1,0:T(8,128)S(1)} %slice.62), channel_id=1, source_target_pairs={{0,16},{16,32},{32,48},{48,0},{1,17},{17,33},{33,49},{49,1},{2,18}... | collective-permute-start | bytes 196616 | tf_op jit(solution)/shard_map/ppermute | solution.py:273
  105.0 14.3 %collective-permute-start.20 = (f32[1024,128]{1,0:T(8,128)S(1)}, f32[1024,128]{1,0:T(8,128)S(1)}, u32[]{:S(2)}, u32[]{:S(2)}) collective-permute-start(f32[1024,128]{1,0:T(8,128)S(1)} %constant_dynamic-update-slice_fusion), channel_id=1, source_target_pairs={{0,192},{64,0},{128,64},{192,128},{1,193},{65,1},{129,65},{193,129... | collective-permute-start | bytes 1572872 | tf_op jit(solution)/shard_map/ppermute | solution.py:273
  108.4 15.1 %collective-permute-start.19 = (f32[1024,128]{1,0:T(8,128)S(1)}, f32[1024,128]{1,0:T(8,128)S(1)}, u32[]{:S(2)}, u32[]{:S(2)}) collective-permute-start(f32[1024,128]{1,0:T(8,128)S(1)} %constant_dynamic-update-slice_fusion), channel_id=1, source_target_pairs={{0,64},{64,128},{128,192},{192,0},{1,65},{65,129},{129,193},{193,1... | collective-permute-start | bytes 1572872 | tf_op jit(solution)/shard_map/ppermute | solution.py:273
  108.5 15.8 %collective-permute-start.28 = (f32[1024,128]{1,0:T(8,128)S(1)}, f32[1024,128]{1,0:T(8,128)S(1)}, u32[]{:S(2)}, u32[]{:S(2)}) collective-permute-start(f32[1024,128]{1,0:T(8,128)S(1)} %constant_dynamic-update-slice_fusion.5), channel_id=1, source_target_pairs={{0,48},{16,0},{32,16},{48,32},{1,49},{17,1},{33,17},{49,33},{2,50}... | collective-permute-start | bytes 1572872 | tf_op jit(solution)/shard_map/ppermute | solution.py:273
  111.8 15.8 %collective-permute-start.27 = (f32[1024,128]{1,0:T(8,128)S(1)}, f32[1024,128]{1,0:T(8,128)S(1)}, u32[]{:S(2)}, u32[]{:S(2)}) collective-permute-start(f32[1024,128]{1,0:T(8,128)S(1)} %constant_dynamic-update-slice_fusion.5), channel_id=1, source_target_pairs={{0,16},{16,32},{32,48},{48,0},{1,17},{17,33},{33,49},{49,1},{2,18}... | collective-permute-start | bytes 1572872 | tf_op jit(solution)/shard_map/ppermute | solution.py:273
  120.1 22.8 %collective-permute-start.22 = (f32[512,128]{1,0:T(8,128)}, f32[512,128]{1,0:T(8,128)S(1)}, u32[]{:S(2)}, u32[]{:S(2)}) collective-permute-start(f32[512,128]{1,0:T(8,128)} %slice.65), channel_id=1, source_target_pairs={{0,192},{64,0},{128,64},{192,128},{1,193},{65,1},{129,65},{193,129... | collective-permute-start | bytes 786440 | tf_op jit(solution)/shard_map/ppermute | solution.py:273
  124.3 18.6 %collective-permute-start.21 = (f32[512,128]{1,0:T(8,128)}, f32[512,128]{1,0:T(8,128)}, u32[]{:S(2)}, u32[]{:S(2)}) collective-permute-start(f32[512,128]{1,0:T(8,128)} %slice.64), channel_id=1, source_target_pairs={{0,64},{64,128},{128,192},{192,0},{1,65},{65,129},{129,193},{193,1... | collective-permute-start | bytes 786440 | tf_op jit(solution)/shard_map/ppermute | solution.py:273
  125.0 17.9 %collective-permute-start.30 = (f32[512,128]{1,0:T(8,128)}, f32[512,128]{1,0:T(8,128)}, u32[]{:S(2)}, u32[]{:S(2)}) collective-permute-start(f32[512,128]{1,0:T(8,128)} %slice.70), channel_id=1, source_target_pairs={{0,48},{16,0},{32,16},{48,32},{1,49},{17,1},{33,17},{49,33},{2,50}... | collective-permute-start | bytes 786440 | tf_op jit(solution)/shard_map/ppermute | solution.py:273
  128.3 14.6 %collective-permute-start.29 = (f32[512,128]{1,0:T(8,128)}, f32[512,128]{1,0:T(8,128)}, u32[]{:S(2)}, u32[]{:S(2)}) collective-permute-start(f32[512,128]{1,0:T(8,128)} %slice.69), channel_id=1, source_target_pairs={{0,16},{16,32},{32,48},{48,0},{1,17},{17,33},{33,49},{49,1},{2,18}... | collective-permute-start | bytes 786440 | tf_op jit(solution)/shard_map/ppermute | solution.py:273
Sparse Core Ops, SparseCore 0:
  64.1 46.3 all-gather.6
  112.3 41.1 all-gather.4

commit v2 on v1

v2 whole, which is shorter than its diff:
```python
import jax
import jax.numpy as jnp
from jax import lax
from jax.experimental import pallas as pl
from jax.experimental.pallas import tpu as pltpu
from jax.sharding import Mesh
from jax.sharding import PartitionSpec as P


NB = 256
ROW = ("y", "x")
COL = ("z", "core")
SLABS = 8
SLAB = NB // SLABS


NT = (((1,), (1,)), ((), ()))
NN = (((1,), (0,)), ((), ()))


def full(left, right, dims=NT):
    return lax.dot_general(left, right, dims, precision=lax.Precision.HIGHEST, preferred_element_type=jnp.float32)


def split(value):
    high = value.astype(jnp.bfloat16)
    return high, (value - high.astype(jnp.float32)).astype(jnp.bfloat16)


def three(left, right, dims=NT):
    def dot(a, b):
        return lax.dot_general(a, b, dims, preferred_element_type=jnp.float32)

    return dot(left[0], right[0]) + dot(left[0], right[1]) + dot(left[1], right[0])


def quick(left, right, dims=NT):
    return three(split(left), split(right), dims)


def pack_kernel(place, matrix, factor, *rest):
    pieces, (buffer, sems) = rest[:SLABS], rest[SLABS:]

    @pl.when(place[2] == 0)
    def _():
        copies = {}
        for tile in range(4):
            for m, source in enumerate((matrix, factor)):
                rows = pl.ds(tile * 8 * NB, 8 * NB)
                copies[tile, m] = pltpu.make_async_copy(source.at[rows], buffer.at[m, rows], sems.at[m * 4 + tile])
                copies[tile, m].start()
        for tile in range(4):
            for m in range(2):
                copies[tile, m].wait()
                for half in range(2):
                    for slab in range(SLABS):
                        value = buffer[m, pl.ds((tile * NB + slab * SLAB) * 8 + half, SLAB, stride=8), :]
                        pieces[slab][pl.ds(((m * 4 + tile) * 2 + half) * SLAB, SLAB), :] = value


def pack(place, matrix, factor):
    return pl.pallas_call(
        pack_kernel,
        in_specs=[pl.BlockSpec(memory_space=pltpu.SMEM)] + [pl.BlockSpec(memory_space=pltpu.HBM)] * 2,
        out_specs=[pl.BlockSpec(memory_space=pltpu.VMEM)] * SLABS,
        out_shape=[jax.ShapeDtypeStruct((16 * SLAB, 128), jnp.float32)] * SLABS,
        scratch_shapes=[pltpu.VMEM((2, 8192, 128), jnp.float32), pltpu.SemaphoreType.DMA((8,))],
        compiler_params=pltpu.CompilerParams(vmem_limit_bytes=40 * 2**20),
        name="pack",
    )(place, far(matrix), far(factor))


def iotas():
    return (
        lax.broadcasted_iota(jnp.int32, (NB, NB), 0),
        lax.broadcasted_iota(jnp.int32, (NB, NB), 1),
    )


def inverses(lowers):
    half = NB // 2
    rows = lax.broadcasted_iota(jnp.int32, (half, NB), 0)
    cols = lax.broadcasted_iota(jnp.int32, (half, NB), 1) % half
    eye = rows == cols
    left = lax.broadcasted_iota(jnp.int32, (half, NB), 1) < half

    def spread(value):
        return jnp.concatenate([jnp.where(left, value, 0.0), jnp.where(left, 0.0, value)], axis=0)

    compact = [jnp.concatenate([lower[:half, :half], lower[half:, half:]], axis=1) for lower in lowers]
    first = []
    for value in compact:
        diagonal = jnp.where(eye, value, 0.0)
        across = 1.0 / jnp.sum(diagonal, axis=0, keepdims=True)
        down = [1.0 / jnp.sum(jnp.where(side, diagonal, 0.0), axis=1, keepdims=True) for side in (left, ~left)]
        down = jnp.where(left, down[0], down[1])
        pair = (rows // 2 == cols // 2) & (rows > cols)
        first.append(jnp.where(eye, across, 0.0) - jnp.where(pair, value * down * across, 0.0))

    def double(level, values):
        step = jnp.right_shift(rows, level) - jnp.right_shift(cols, level)
        band = (step == 1) & (jnp.right_shift(rows, level + 1) == jnp.right_shift(cols, level + 1))
        blocks = [quick(value, spread(jnp.where(band, whole, 0.0)), NN) for value, whole in zip(values, compact)]
        return tuple(value - quick(block, spread(value), NN) for value, block in zip(values, blocks))

    values = lax.fori_loop(1, 7, double, tuple(first))
    out = []
    for value, lower in zip(values, lowers):
        top, low = value[:, :half], value[:, half:]
        corner = quick(quick(low, lower[half:, :half], NN), top, NN)
        result = jnp.concatenate([jnp.where(left, value, 0.0), jnp.concatenate([-corner, low], axis=1)], axis=0)
        diag_rows, diag_cols = iotas()
        rest = jnp.where(diag_rows == diag_cols, 1.0, 0.0) - full(lower, result, NN)
        out.append(result + quick(result, rest, NN))
    return out


def head_math(tile, head_hi, head_lo, cores):
    a00, l00, a10, low, a11, l11 = (tile(*k) for k in ((0, 0, 0), (0, 0, 1), (0, 1, 0), (0, 1, 1), (1, 1, 0), (1, 1, 1)))
    rows, cols = iotas()
    eye = rows == cols

    def keep(k, value):
        head_hi[k], head_lo[k] = split(value)
        return head_hi[k], head_lo[k]

    inv0, inv1 = inverses((l00, l11))
    inv0, inv1, low = keep(0, inv0), keep(2, inv1), keep(5, low)
    part = three(split(three(inv0, split(jnp.where(eye, 0.5 * a00, a00)), NN)), inv0)
    cores[0] = part + part.T
    half0 = keep(4, three(split(a10), inv0) - 0.5 * three(low, keep(1, cores[0])))
    inner = jnp.where(eye, 0.5 * a11, a11) - three(half0, low)
    part = three(split(three(inv1, split(inner), NN)), inv1)
    cores[1] = part + part.T
    keep(3, cores[1])


def main_kernel(place, raw_far, local_far, *rest):
    grids, rest = rest[:10], rest[10:]
    out, raw_row, raw_col, local, head, cores, col_hi, col_lo, head_hi, head_lo, sems = rest
    step = pl.program_id(0)
    p = place[0]
    c = place[1]

    def load_local(tile):
        return pltpu.make_async_copy(local_far.at[pl.ds(tile * 2048, 2048)], local.at[tile], sems.at[tile])

    def read(raw, core, m, tile):
        at = (m * 4 + tile) * 2
        return jnp.concatenate([raw[:, core, at + half].reshape(NB, 128) for half in range(2)], axis=1)

    def panels(raw, tile):
        def heads(k):
            return head_hi[k], head_lo[k]

        a0, a1 = read(raw, 0, 0, tile), read(raw, 1, 0, tile)
        f0, f1 = split(read(raw, 0, 1, tile)), split(read(raw, 1, 1, tile))
        p0 = three(f0, heads(1))
        half0 = three(split(a0), heads(0)) - 0.5 * p0
        g0 = split(half0)
        a1 = a1 - three(g0, heads(5)) - three(f0, heads(4))
        p1 = three(f1, heads(3))
        half1 = three(split(a1), heads(2)) - 0.5 * p1
        g1 = split(half1)
        return g0, f0, g1, f1, half0 - 0.5 * p0, half1 - 0.5 * p1

    @pl.when(step == 0)
    def _():
        load_row = pltpu.make_async_copy(raw_far.at[:, :, pl.ds(0, 16)], raw_row, sems.at[4])
        load_head = pltpu.make_async_copy(raw_far.at[:, :, pl.ds(16, 8)], head, sems.at[5])
        load_head.start()
        load_row.start()
        for tile in range(4):
            load_local(tile).start()
        y, x = p // 4, p % 4
        loads = []

        def spot(dy, dx):
            return (((y + dy) % 4) * 4 + (x + dx) % 4 + 16 - c) % 16

        for m in range(2):
            near, back, ahead, far_one, far_two = grids[5 * m : 5 * m + 5]
            order = (0, 3, 1, 2)
            for k in range(4):
                for part, dy in ((near, 0), (back, 3), (ahead, 1), (far_one if k < 2 else far_two, 2)):
                    dx = order[k]
                    at = spot(dy, dx) if m == 0 else spot(dx, dy)
                    if dy == 2:
                        slot = raw_col.at[at // 2, at % 2, pl.ds(8 * m, 8)]
                        loads.append(pltpu.make_async_copy(part.at[k % 2], slot, sems.at[6 + 4 * m + k]))
                        loads[-1].start()
                    else:
                        raw_col[at // 2, at % 2, 8 * m : 8 * m + 8] = part[k]
        load_head.wait()

        def square(core, row, m):
            at = (row * 2 + m) * 2
            return jnp.concatenate([head[:, core, at + half].reshape(NB, 128) for half in range(2)], axis=1)

        head_math(square, head_hi, head_lo, cores)
        for load in loads:
            load.wait()

        def one(tile, carry):
            g0, f0, g1, f1, _, _ = panels(raw_col, tile)
            for k, (hi, lo) in enumerate((f0, g0, f1, g1)):
                col_hi[tile, :, k * NB : (k + 1) * NB] = hi
                col_lo[tile, :, k * NB : (k + 1) * NB] = lo
            return carry

        lax.fori_loop(0, 4, one, 0)
        load_row.wait()

    g0, f0, g1, f1, done0, done1 = panels(raw_row, step)
    load_local(step).wait()
    row_hi = jnp.concatenate([g0[0], f0[0], g1[0], f1[0]], axis=1)
    row_lo = jnp.concatenate([g0[1], f0[1], g1[1], f1[1]], axis=1)
    rows, cols = iotas()

    def put(tile, value):
        for half in range(2):
            out[pl.ds(tile * 2 + half, NB, stride=8), :] = value[:, half * 128 : (half + 1) * 128]

    def get(tile):
        return jnp.concatenate([local[step, pl.ds(tile * 2 + half, NB, stride=8), :] for half in range(2)], axis=1)

    def update(tile, carry):
        below = (step > tile) | ((step == tile) & (p > c))
        same = (step == tile) & (p == c)
        ours = (below | same) & ((tile > 0) | (c > 1))

        @pl.when(ours)
        def _():
            change = three((row_hi, row_lo), (col_hi[tile], col_lo[tile]))
            keep = jnp.logical_or(below, rows >= cols)
            put(tile, get(tile) - jnp.where(keep, change, 0.0))

        @pl.when(jnp.logical_not(ours))
        def _():
            put(tile, get(tile))

        return carry

    lax.fori_loop(0, 4, update, 0)
    top = step * 16 + p
    for block, done in enumerate((done0, done1)):

        @pl.when((c == block) & (top > block))
        def _():
            put(0, done)

        @pl.when((c == block) & (top == block))
        def _():
            put(0, jnp.where(rows >= cols, cores[block], 0.0))


def main_math(place, raw_row, grids, local):
    raw = (SLABS, 2, 16, SLAB, 128)
    vmem = pl.BlockSpec(memory_space=pltpu.VMEM)
    hbm = pl.BlockSpec(memory_space=pltpu.HBM)
    grids = [part.reshape(-1, 8, SLAB, 128) for part in grids]
    grids = [far(part) if k % 5 > 2 else part for k, part in enumerate(grids)]
    places = [hbm if k % 5 > 2 else vmem for k in range(10)]
    return pl.pallas_call(
        main_kernel,
        grid=(4,),
        in_specs=[pl.BlockSpec(memory_space=pltpu.SMEM), hbm, hbm] + places,
        out_specs=pl.BlockSpec((2048, 128), lambda i: (i, 0)),
        out_shape=jax.ShapeDtypeStruct((8192, 128), jnp.float32),
        scratch_shapes=[
            pltpu.VMEM(raw, jnp.float32),
            pltpu.VMEM(raw, jnp.float32),
            pltpu.VMEM((4, 2048, 128), jnp.float32),
            pltpu.VMEM((SLABS, 2, 8, SLAB, 128), jnp.float32),
            pltpu.VMEM((2, NB, NB), jnp.float32),
            pltpu.VMEM((4, NB, 4 * NB), jnp.bfloat16),
            pltpu.VMEM((4, NB, 4 * NB), jnp.bfloat16),
            pltpu.VMEM((6, NB, NB), jnp.bfloat16),
            pltpu.VMEM((6, NB, NB), jnp.bfloat16),
            pltpu.SemaphoreType.DMA((14,)),
        ],
        compiler_params=pltpu.CompilerParams(vmem_limit_bytes=32 * 2**20),
        name="main",
    )(place, far(raw_row.reshape(SLABS, 2, 24, SLAB, 128)), far(local), *grids)


def shift(value, axis, size, by):
    return lax.ppermute(value, axis, [(i, (i + by) % size) for i in range(size)])


def far(value):
    return pltpu.with_memory_space_constraint(value, pltpu.HBM)


def ring4(value, axis):
    up, down = shift(value, axis, 4, 1), shift(value, axis, 4, -1)
    half = value.shape[0] // 2
    return [value, up, down, shift(up[:half], axis, 4, 1), shift(down[half:], axis, 4, -1)]


def device(matrix, factor):
    x, y, z, _ = (lax.axis_index(name) for name in ("x", "y", "z", "core"))
    p = lax.axis_index(ROW)
    c = lax.axis_index(COL)
    place = jnp.stack([p, c, z])
    local = matrix.reshape(8192, 128)
    pieces = pack(place, local, factor.reshape(8192, 128))
    order = (4, 1, 7, 2, 6, 3, 5)
    got = [lax.ppermute(pieces[k], "z", [(0, k)]) for k in order]
    total = got[0]
    for value in got[1:]:
        total = total + value
    mine = jnp.where(z == 0, pieces[0], total)
    moved = lax.ppermute(mine, ROW + COL, [(r * 16 + j, (j + r) % 16 * 16 + j) for r in range(16) for j in range(16)])
    swapped = lax.ppermute(moved, ROW + COL, [(q * 16 + j, q * 16 + (q - j) % 16) for q in range(16) for j in range(16)])

    top = mine.reshape(2, 4, 2 * SLAB, 128)[:, 0].reshape(4 * SLAB, 128)
    across = lax.ppermute(top, ROW, [(0, 1), (1, 0)])
    tops = jnp.concatenate([jnp.where(p == 0, top, across), jnp.where(p == 0, across, top)], 0)
    sent = lax.ppermute(tops, ROW, [(0, 3), (1, 2)])
    tops = jnp.where(x < 2, tops, sent)
    sent = [lax.ppermute(tops, "y", [(0, k)]) for k in (2, 1, 3)]
    tops = jnp.where(y == 0, tops, sent[0] + sent[1] + sent[2])
    raw_row = lax.all_gather(jnp.concatenate([mine, tops], 0), COL)

    first = ring4(swapped[: 8 * SLAB], "x")
    second = ring4(swapped[8 * SLAB :], "y")
    grids = ring4(jnp.concatenate(first, 0), "y") + ring4(jnp.concatenate(second, 0), "x")
    return main_math(place, raw_row, grids, local).reshape(matrix.shape)


def solution(mesh):
    torus = Mesh(mesh.devices.reshape(4, 4, 8, 2), ("y", "x", "z", "core"))
    spec = P(None, ROW, None, None, COL, None)
    return jax.shard_map(device, mesh=torus, in_specs=(spec, spec), out_specs=spec, check_vma=False)
```

time: 179 us -> 160 us (0.89)
  the two profiles are of different devices: /device:TPU:2 before, /device:TPU:120 now
where the time goes in v2:
time: 160 us
  waiting for transfers between devices  60.3 us (38%)
  starting transfers between devices  58.6 us (37%)
  Pallas kernels  26 us (16%)
  between operations  13.8 us (9%)
    ppermute x16, starting transfers between devices, shift(): lax.ppermute(value, axis, [(i, (i + by) % size) for i in range(size)])  41.1 us
    ppermute x7, waiting for transfers between devices, device(): got = [lax.ppermute(pieces[k], 'z', [(0, k)]) for k in order]  25.7 us
    pallas_call x1, Pallas kernels, main_math(): pl.pallas_call(main_kernel, grid=(4,), in_specs=[pl.BlockSpec(memory_spac...  25.3 us
    ppermute x16, waiting for transfers between devices, shift(): lax.ppermute(value, axis, [(i, (i + by) % size) for i in range(size)])  19.4 us
    ppermute x3, waiting for transfers between devices, device(): sent = [lax.ppermute(tops, 'y', [(0, k)]) for k in (2, 1, 3)]  10.4 us
    ppermute x1, starting transfers between devices, device(): lax.ppermute(mine, ROW + COL, [(r * 16 + j, (j + r) % 16 * 16 + j) for r...  7.57 us
    ppermute x7, starting transfers between devices, device(): got = [lax.ppermute(pieces[k], 'z', [(0, k)]) for k in order]  5.36 us
    ppermute x1, waiting for transfers between devices, device(): lax.ppermute(mine, ROW + COL, [(r * 16 + j, (j + r) % 16 * 16 + j) for r...  4.85 us
  transfers between devices with their start and end apart: 31, of which 8 were waited for; matrix products, arithmetic and copies ran while one was open for 0% of the time, Pallas kernels for 0%

profile of v2, /device:TPU:120, one launch (start us, length us, event | category | flops | bytes accessed | tf_op | source)
XLA Modules:
  0.0 160.0 jit_solution(18221019945263542673)
XLA Ops:
  6.5 0.1 pad_add_fusion.place
  6.6 0.6 pack.1
  7.2 0.7 collective-permute-start
  7.9 0.7 collective-permute-start.1
  8.6 0.7 collective-permute-start.2
  9.3 0.7 collective-permute-start.3
  10.0 0.7 collective-permute-start.4
  10.7 0.0 collective-permute-done
  10.7 1.3 collective-permute-start.5
  12.0 0.0 collective-permute-done.1
  12.0 0.7 collective-permute-start.6
  12.7 0.0 collective-permute-done.2
  12.7 0.0 collective-permute-done.3
  12.7 0.0 collective-permute-done.4
  12.7 25.7 %collective-permute-done.5 = f32[512,128]{1,0:T(8,128)S(1)} collective-permute-done((f32[512,128]{1,0:T(8,128)S(1)}, f32[512,128]{1,0:T(8,128)S(1)}, u32[]{:S(2)}, u32[]{:S(2)}) %collective-permute-start.5) | collective-permute-done | bytes 262176 | tf_op jit(solution)/shard_map/ppermute | solution.py:309
  38.4 0.0 collective-permute-done.6
  38.4 0.1 add_select_fusion
  38.5 0.7 collective-permute-start.7
  39.2 0.0 collective-permute-done.7
  39.3 0.7 collective-permute-start.8
  39.9 0.0 collective-permute-done.8
  40.0 1.3 collective-permute-start.11
  41.3 0.7 collective-permute-start.10
  41.9 0.7 collective-permute-start.9
  42.6 10.4 %collective-permute-done.11 = f32[256,128]{1,0:T(8,128)S(1)} collective-permute-done((f32[256,128]{1,0:T(8,128)S(1)}, f32[256,128]{1,0:T(8,128)S(1)}, u32[]{:S(2)}, u32[]{:S(2)}) %collective-permute-start.11) | collective-permute-done | bytes 131104 | tf_op jit(solution)/shard_map/ppermute | solution.py:322
  53.0 0.0 collective-permute-done.10
  53.0 0.0 collective-permute-done.9
  53.0 0.8 pad_maximum_fusion
  53.8 0.0 all-gather.3.cloned.1.call-update
  53.8 7.6 %collective-permute-start.12 = (f32[512,128]{1,0:T(8,128)S(1)}, f32[512,128]{1,0:T(8,128)S(1)}, u32[]{:S(2)}, u32[]{:S(2)}) collective-permute-start(f32[512,128]{1,0:T(8,128)S(1)} %add_select_fusion), channel_id=1, source_target_pairs={{0,0},{1,17},{2,34},{3,51},{4,68},{5,85},{6,102},{7,119},{8,136},{... | collective-permute-start | bytes 786440 | tf_op jit(solution)/shard_map/ppermute | solution.py:314
  61.4 4.9 %collective-permute-done.12 = f32[512,128]{1,0:T(8,128)S(1)} collective-permute-done((f32[512,128]{1,0:T(8,128)S(1)}, f32[512,128]{1,0:T(8,128)S(1)}, u32[]{:S(2)}, u32[]{:S(2)}) %collective-permute-start.12) | collective-permute-done | bytes 262176 | tf_op jit(solution)/shard_map/ppermute | solution.py:314
  66.3 0.7 collective-permute-start.13
  66.9 0.0 collective-permute-done.13
  67.0 18.2 %collective-permute-start.23 = (f32[256,128]{1,0:T(8,128)S(1)}, f32[256,128]{1,0:T(8,128)S(1)}, u32[]{:S(2)}, u32[]{:S(2)}) collective-permute-start(f32[256,128]{1,0:T(8,128)S(1)} %get-tuple-element.21), channel_id=1, source_target_pairs={{0,192},{64,0},{128,64},{192,128},{1,193},{65,1},{129,65},{193,129... | collective-permute-start | bytes 393224 | tf_op jit(solution)/shard_map/ppermute | solution.py:288
  85.2 0.0 collective-permute-start.22
  85.2 5.0 %collective-permute-start.15 = (f32[256,128]{1,0:T(8,128)S(1)}, f32[256,128]{1,0:T(8,128)S(1)}, u32[]{:S(2)}, u32[]{:S(2)}) collective-permute-start(f32[256,128]{1,0:T(8,128)S(1)} %get-tuple-element.24), channel_id=1, source_target_pairs={{0,48},{16,0},{32,16},{48,32},{1,49},{17,1},{33,17},{49,33},{2,50}... | collective-permute-start | bytes 393224 | tf_op jit(solution)/shard_map/ppermute | solution.py:288
  90.1 0.0 collective-permute-start.14
  90.1 0.0 collective-permute-done.23
  90.2 0.1 collective-permute-start.25
  90.2 0.0 collective-permute-done.22
  90.3 3.3 %collective-permute-start.24 = (f32[128,128]{1,0:T(8,128)S(1)}, f32[128,128]{1,0:T(8,128)S(1)}, u32[]{:S(2)}, u32[]{:S(2)}) collective-permute-start(f32[128,128]{1,0:T(8,128)S(1)} %slice.51), channel_id=1, source_target_pairs={{0,64},{64,128},{128,192},{192,0},{1,65},{65,129},{129,193},{193,1... | collective-permute-start | bytes 196616 | tf_op jit(solution)/shard_map/ppermute | solution.py:288
  93.6 0.0 collective-permute-done.15
  93.6 3.3 %collective-permute-start.17 = (f32[128,128]{1,0:T(8,128)S(1)}, f32[128,128]{1,0:T(8,128)S(1)}, u32[]{:S(2)}, u32[]{:S(2)}) collective-permute-start(f32[128,128]{1,0:T(8,128)S(1)} %slice.47), channel_id=1, source_target_pairs={{0,48},{16,0},{32,16},{48,32},{1,49},{17,1},{33,17},{49,33},{2,50}... | collective-permute-start | bytes 196616 | tf_op jit(solution)/shard_map/ppermute | solution.py:288
  96.9 0.0 collective-permute-done.14
  96.9 0.1 collective-permute-start.16
  97.1 6.1 %collective-permute-done.16 = f32[128,128]{1,0:T(8,128)S(1)} collective-permute-done((f32[128,128]{1,0:T(8,128)S(1)}, f32[128,128]{1,0:T(8,128)S(1)}, u32[]{:S(2)}, u32[]{:S(2)}) %collective-permute-start.16) | collective-permute-done | bytes 65568 | tf_op jit(solution)/shard_map/ppermute | solution.py:288
  103.2 0.0 collective-permute-done.17
  103.2 0.1 collective-permute-start.19
  103.3 3.2 %collective-permute-start.18 = (f32[1024,128]{1,0:T(8,128)S(1)}, f32[1024,128]{1,0:T(8,128)S(1)}, u32[]{:S(2)}, u32[]{:S(2)}) collective-permute-start(f32[1024,128]{1,0:T(8,128)S(1)} %constant_dynamic-update-slice_fusion), channel_id=1, source_target_pairs={{0,64},{64,128},{128,192},{192,0},{1,65},{65,129},{129,193},{193,1... | collective-permute-start | bytes 1572872 | tf_op jit(solution)/shard_map/ppermute | solution.py:288
  106.5 0.0 collective-permute-done.24
  106.5 0.0 collective-permute-done.25
  106.5 0.1 collective-permute-start.27
  106.6 2.0 %collective-permute-start.26 = (f32[1024,128]{1,0:T(8,128)S(1)}, f32[1024,128]{1,0:T(8,128)S(1)}, u32[]{:S(2)}, u32[]{:S(2)}) collective-permute-start(f32[1024,128]{1,0:T(8,128)S(1)} %constant_dynamic-update-slice_fusion.5), channel_id=1, source_target_pairs={{0,16},{16,32},{32,48},{48,0},{1,17},{17,33},{33,49},{49,1},{2,18}... | collective-permute-start | bytes 1572872 | tf_op jit(solution)/shard_map/ppermute | solution.py:288
  108.6 7.1 %collective-permute-done.19 = f32[1024,128]{1,0:T(8,128)S(1)} collective-permute-done((f32[1024,128]{1,0:T(8,128)S(1)}, f32[1024,128]{1,0:T(8,128)S(1)}, u32[]{:S(2)}, u32[]{:S(2)}) %collective-permute-start.19) | collective-permute-done | bytes 524320 | tf_op jit(solution)/shard_map/ppermute | solution.py:288
  115.8 0.3 collective-permute-start.21
  116.1 0.0 collective-permute-done.18
  116.1 3.3 %collective-permute-start.20 = (f32[512,128]{1,0:T(8,128)S(1)}, f32[512,128]{1,0:T(8,128)}, u32[]{:S(2)}, u32[]{:S(2)}) collective-permute-start(f32[512,128]{1,0:T(8,128)S(1)} %slice.48), channel_id=1, source_target_pairs={{0,64},{64,128},{128,192},{192,0},{1,65},{65,129},{129,193},{193,1... | collective-permute-start | bytes 786440 | tf_op jit(solution)/shard_map/ppermute | solution.py:288
  119.4 0.0 collective-permute-done.27
  119.4 0.6 collective-permute-start.29
  120.0 1.6 %collective-permute-start.28 = (f32[512,128]{1,0:T(8,128)S(1)}, f32[512,128]{1,0:T(8,128)}, u32[]{:S(2)}, u32[]{:S(2)}) collective-permute-start(f32[512,128]{1,0:T(8,128)S(1)} %slice.53), channel_id=1, source_target_pairs={{0,16},{16,32},{32,48},{48,0},{1,17},{17,33},{33,49},{49,1},{2,18}... | collective-permute-start | bytes 786440 | tf_op jit(solution)/shard_map/ppermute | solution.py:288
  121.6 2.0 %collective-permute-done.21 = f32[512,128]{1,0:T(8,128)S(1)} collective-permute-done((f32[512,128]{1,0:T(8,128)S(1)}, f32[512,128]{1,0:T(8,128)S(1)}, u32[]{:S(2)}, u32[]{:S(2)}) %collective-permute-start.21) | collective-permute-done | bytes 262176 | tf_op jit(solution)/shard_map/ppermute | solution.py:288
  123.6 2.3 %collective-permute-done.29 = f32[512,128]{1,0:T(8,128)} collective-permute-done((f32[512,128]{1,0:T(8,128)S(1)}, f32[512,128]{1,0:T(8,128)}, u32[]{:S(2)}, u32[]{:S(2)}) %collective-permute-start.29) | collective-permute-done | bytes 262176 | tf_op jit(solution)/shard_map/ppermute | solution.py:288
  126.0 1.8 %collective-permute-done.28 = f32[512,128]{1,0:T(8,128)} collective-permute-done((f32[512,128]{1,0:T(8,128)S(1)}, f32[512,128]{1,0:T(8,128)}, u32[]{:S(2)}, u32[]{:S(2)}) %collective-permute-start.28) | collective-permute-done | bytes 262176 | tf_op jit(solution)/shard_map/ppermute | solution.py:288
  127.8 25.3 %main.1 = f32[8192,128]{1,0:T(8,128)} custom-call(s32[3]{0:T(128)S(1)} %pad_add_fusion.place, f32[8,2,24,32,128]{4,3,2,1,0:T(8,128)} %bitcast.31, f32[8192,128]{1,0:T(8,128)} %bitcast.30, f32[4,8,32,128]{3,2,1,0:T(8,128)S(1)} %bitcast.27, f32[4,8,32,128]{3,2,1,0:T(8,128)S(1)} %bitcast.24, f32[4,8,32,128]{3,2,1,0:T(8,128)S(1)} %bitcast.23, ...), custom_call_target="tpu_custom_call" | custom-call | tf_op jit(solution)/shard_map/main/pallas_call | solution.py:264
  (28 shorter events, 0.3 us)
Async XLA Ops:
  6.5 121.2 %all-gather.3.cloned.1.call-start = ((), (), s32[]{:S(2)}) async-start(), calls=%async_computation | async-start | bytes 6684672 | tf_op jit(solution)/shard_map/all_gather | solution.py:324
  7.2 3.4 %collective-permute-start = (f32[512,128]{1,0:T(8,128)S(1)}, f32[512,128]{1,0:T(8,128)S(1)}, u32[]{:S(2)}, u32[]{:S(2)}) collective-permute-start(f32[512,128]{1,0:T(8,128)S(1)} %get-tuple-element.14), channel_id=1, source_target_pairs={{0,8},{1,9},{16,24},{17,25},{32,40},{33,41},{48,56},{49,57},{64,72... | collective-permute-start | bytes 786440 | tf_op jit(solution)/shard_map/ppermute | solution.py:309
  7.9 4.1 %collective-permute-start.1 = (f32[512,128]{1,0:T(8,128)S(1)}, f32[512,128]{1,0:T(8,128)S(1)}, u32[]{:S(2)}, u32[]{:S(2)}) collective-permute-start(f32[512,128]{1,0:T(8,128)S(1)} %get-tuple-element.15), channel_id=1, source_target_pairs={{0,2},{1,3},{16,18},{17,19},{32,34},{33,35},{48,50},{49,51},{64,66... | collective-permute-start | bytes 786440 | tf_op jit(solution)/shard_map/ppermute | solution.py:309
  8.6 4.1 %collective-permute-start.2 = (f32[512,128]{1,0:T(8,128)S(1)}, f32[512,128]{1,0:T(8,128)S(1)}, u32[]{:S(2)}, u32[]{:S(2)}) collective-permute-start(f32[512,128]{1,0:T(8,128)S(1)} %get-tuple-element.16), channel_id=1, source_target_pairs={{0,14},{1,15},{16,30},{17,31},{32,46},{33,47},{48,62},{49,63},{64,... | collective-permute-start | bytes 786440 | tf_op jit(solution)/shard_map/ppermute | solution.py:309
  9.3 3.4 %collective-permute-start.3 = (f32[512,128]{1,0:T(8,128)S(1)}, f32[512,128]{1,0:T(8,128)S(1)}, u32[]{:S(2)}, u32[]{:S(2)}) collective-permute-start(f32[512,128]{1,0:T(8,128)S(1)} %get-tuple-element.17), channel_id=1, source_target_pairs={{0,4},{1,5},{16,20},{17,21},{32,36},{33,37},{48,52},{49,53},{64,68... | collective-permute-start | bytes 786440 | tf_op jit(solution)/shard_map/ppermute | solution.py:309
  10.0 2.7 %collective-permute-start.4 = (f32[512,128]{1,0:T(8,128)S(1)}, f32[512,128]{1,0:T(8,128)S(1)}, u32[]{:S(2)}, u32[]{:S(2)}) collective-permute-start(f32[512,128]{1,0:T(8,128)S(1)} %get-tuple-element.18), channel_id=1, source_target_pairs={{0,12},{1,13},{16,28},{17,29},{32,44},{33,45},{48,60},{49,61},{64,... | collective-permute-start | bytes 786440 | tf_op jit(solution)/shard_map/ppermute | solution.py:309
  10.7 27.7 %collective-permute-start.5 = (f32[512,128]{1,0:T(8,128)S(1)}, f32[512,128]{1,0:T(8,128)S(1)}, u32[]{:S(2)}, u32[]{:S(2)}) collective-permute-start(f32[512,128]{1,0:T(8,128)S(1)} %get-tuple-element.19), channel_id=1, source_target_pairs={{0,6},{1,7},{16,22},{17,23},{32,38},{33,39},{48,54},{49,55},{64,70... | collective-permute-start | bytes 786440 | tf_op jit(solution)/shard_map/ppermute | solution.py:309
  12.0 26.4 %collective-permute-start.6 = (f32[512,128]{1,0:T(8,128)S(1)}, f32[512,128]{1,0:T(8,128)S(1)}, u32[]{:S(2)}, u32[]{:S(2)}) collective-permute-start(f32[512,128]{1,0:T(8,128)S(1)} %get-tuple-element.20), channel_id=1, source_target_pairs={{0,10},{1,11},{16,26},{17,27},{32,42},{33,43},{48,58},{49,59},{64,... | collective-permute-start | bytes 786440 | tf_op jit(solution)/shard_map/ppermute | solution.py:309
  38.5 0.7 collective-permute-start.7
  39.3 0.7 collective-permute-start.8
  40.0 13.0 %collective-permute-start.11 = (f32[256,128]{1,0:T(8,128)S(1)}, f32[256,128]{1,0:T(8,128)S(1)}, u32[]{:S(2)}, u32[]{:S(2)}) collective-permute-start(f32[256,128]{1,0:T(8,128)S(1)} %broadcast_select_fusion), channel_id=1, source_target_pairs={{0,192},{1,193},{2,194},{3,195},{4,196},{5,197},{6,198},{7,199},{8... | collective-permute-start | bytes 393224 | tf_op jit(solution)/shard_map/ppermute | solution.py:322
  41.3 11.7 %collective-permute-start.10 = (f32[256,128]{1,0:T(8,128)S(1)}, f32[256,128]{1,0:T(8,128)S(1)}, u32[]{:S(2)}, u32[]{:S(2)}) collective-permute-start(f32[256,128]{1,0:T(8,128)S(1)} %broadcast_select_fusion), channel_id=1, source_target_pairs={{0,64},{1,65},{2,66},{3,67},{4,68},{5,69},{6,70},{7,71},{8,72},{9,... | collective-permute-start | bytes 393224 | tf_op jit(solution)/shard_map/ppermute | solution.py:322
  41.9 11.0 %collective-permute-start.9 = (f32[256,128]{1,0:T(8,128)S(1)}, f32[256,128]{1,0:T(8,128)S(1)}, u32[]{:S(2)}, u32[]{:S(2)}) collective-permute-start(f32[256,128]{1,0:T(8,128)S(1)} %broadcast_select_fusion), channel_id=1, source_target_pairs={{0,128},{1,129},{2,130},{3,131},{4,132},{5,133},{6,134},{7,135},{8... | collective-permute-start | bytes 393224 | tf_op jit(solution)/shard_map/ppermute | solution.py:322
  53.8 12.4 %collective-permute-start.12 = (f32[512,128]{1,0:T(8,128)S(1)}, f32[512,128]{1,0:T(8,128)S(1)}, u32[]{:S(2)}, u32[]{:S(2)}) collective-permute-start(f32[512,128]{1,0:T(8,128)S(1)} %add_select_fusion), channel_id=1, source_target_pairs={{0,0},{1,17},{2,34},{3,51},{4,68},{5,85},{6,102},{7,119},{8,136},{... | collective-permute-start | bytes 786440 | tf_op jit(solution)/shard_map/ppermute | solution.py:314
  66.3 0.7 collective-permute-start.13
  67.0 23.2 %collective-permute-start.23 = (f32[256,128]{1,0:T(8,128)S(1)}, f32[256,128]{1,0:T(8,128)S(1)}, u32[]{:S(2)}, u32[]{:S(2)}) collective-permute-start(f32[256,128]{1,0:T(8,128)S(1)} %get-tuple-element.21), channel_id=1, source_target_pairs={{0,192},{64,0},{128,64},{192,128},{1,193},{65,1},{129,65},{193,129... | collective-permute-start | bytes 393224 | tf_op jit(solution)/shard_map/ppermute | solution.py:288
  85.2 5.1 %collective-permute-start.22 = (f32[256,128]{1,0:T(8,128)S(1)}, f32[256,128]{1,0:T(8,128)S(1)}, u32[]{:S(2)}, u32[]{:S(2)}) collective-permute-start(f32[256,128]{1,0:T(8,128)S(1)} %get-tuple-element.21), channel_id=1, source_target_pairs={{0,64},{64,128},{128,192},{192,0},{1,65},{65,129},{129,193},{193,1... | collective-permute-start | bytes 393224 | tf_op jit(solution)/shard_map/ppermute | solution.py:288
  85.2 8.4 %collective-permute-start.15 = (f32[256,128]{1,0:T(8,128)S(1)}, f32[256,128]{1,0:T(8,128)S(1)}, u32[]{:S(2)}, u32[]{:S(2)}) collective-permute-start(f32[256,128]{1,0:T(8,128)S(1)} %get-tuple-element.24), channel_id=1, source_target_pairs={{0,48},{16,0},{32,16},{48,32},{1,49},{17,1},{33,17},{49,33},{2,50}... | collective-permute-start | bytes 393224 | tf_op jit(solution)/shard_map/ppermute | solution.py:288
  90.1 6.7 %collective-permute-start.14 = (f32[256,128]{1,0:T(8,128)S(1)}, f32[256,128]{1,0:T(8,128)S(1)}, u32[]{:S(2)}, u32[]{:S(2)}) collective-permute-start(f32[256,128]{1,0:T(8,128)S(1)} %get-tuple-element.24), channel_id=1, source_target_pairs={{0,16},{16,32},{32,48},{48,0},{1,17},{17,33},{33,49},{49,1},{2,18}... | collective-permute-start | bytes 393224 | tf_op jit(solution)/shard_map/ppermute | solution.py:288
  90.2 16.3 %collective-permute-start.25 = (f32[128,128]{1,0:T(8,128)S(1)}, f32[128,128]{1,0:T(8,128)S(1)}, u32[]{:S(2)}, u32[]{:S(2)}) collective-permute-start(f32[128,128]{1,0:T(8,128)S(1)} %slice.52), channel_id=1, source_target_pairs={{0,192},{64,0},{128,64},{192,128},{1,193},{65,1},{129,65},{193,129... | collective-permute-start | bytes 196616 | tf_op jit(solution)/shard_map/ppermute | solution.py:288
  90.3 16.2 %collective-permute-start.24 = (f32[128,128]{1,0:T(8,128)S(1)}, f32[128,128]{1,0:T(8,128)S(1)}, u32[]{:S(2)}, u32[]{:S(2)}) collective-permute-start(f32[128,128]{1,0:T(8,128)S(1)} %slice.51), channel_id=1, source_target_pairs={{0,64},{64,128},{128,192},{192,0},{1,65},{65,129},{129,193},{193,1... | collective-permute-start | bytes 196616 | tf_op jit(solution)/shard_map/ppermute | solution.py:288
  93.6 9.6 %collective-permute-start.17 = (f32[128,128]{1,0:T(8,128)S(1)}, f32[128,128]{1,0:T(8,128)S(1)}, u32[]{:S(2)}, u32[]{:S(2)}) collective-permute-start(f32[128,128]{1,0:T(8,128)S(1)} %slice.47), channel_id=1, source_target_pairs={{0,48},{16,0},{32,16},{48,32},{1,49},{17,1},{33,17},{49,33},{2,50}... | collective-permute-start | bytes 196616 | tf_op jit(solution)/shard_map/ppermute | solution.py:288
  96.9 6.3 %collective-permute-start.16 = (f32[128,128]{1,0:T(8,128)S(1)}, f32[128,128]{1,0:T(8,128)S(1)}, u32[]{:S(2)}, u32[]{:S(2)}) collective-permute-start(f32[128,128]{1,0:T(8,128)S(1)} %slice.46), channel_id=1, source_target_pairs={{0,16},{16,32},{32,48},{48,0},{1,17},{17,33},{33,49},{49,1},{2,18}... | collective-permute-start | bytes 196616 | tf_op jit(solution)/shard_map/ppermute | solution.py:288
  103.2 12.6 %collective-permute-start.19 = (f32[1024,128]{1,0:T(8,128)S(1)}, f32[1024,128]{1,0:T(8,128)S(1)}, u32[]{:S(2)}, u32[]{:S(2)}) collective-permute-start(f32[1024,128]{1,0:T(8,128)S(1)} %constant_dynamic-update-slice_fusion), channel_id=1, source_target_pairs={{0,192},{64,0},{128,64},{192,128},{1,193},{65,1},{129,65},{193,129... | collective-permute-start | bytes 1572872 | tf_op jit(solution)/shard_map/ppermute | solution.py:288
  103.3 12.8 %collective-permute-start.18 = (f32[1024,128]{1,0:T(8,128)S(1)}, f32[1024,128]{1,0:T(8,128)S(1)}, u32[]{:S(2)}, u32[]{:S(2)}) collective-permute-start(f32[1024,128]{1,0:T(8,128)S(1)} %constant_dynamic-update-slice_fusion), channel_id=1, source_target_pairs={{0,64},{64,128},{128,192},{192,0},{1,65},{65,129},{129,193},{193,1... | collective-permute-start | bytes 1572872 | tf_op jit(solution)/shard_map/ppermute | solution.py:288
  106.5 12.9 %collective-permute-start.27 = (f32[1024,128]{1,0:T(8,128)S(1)}, f32[1024,128]{1,0:T(8,128)S(1)}, u32[]{:S(2)}, u32[]{:S(2)}) collective-permute-start(f32[1024,128]{1,0:T(8,128)S(1)} %constant_dynamic-update-slice_fusion.5), channel_id=1, source_target_pairs={{0,48},{16,0},{32,16},{48,32},{1,49},{17,1},{33,17},{49,33},{2,50}... | collective-permute-start | bytes 1572872 | tf_op jit(solution)/shard_map/ppermute | solution.py:288
  106.6 13.4 %collective-permute-start.26 = (f32[1024,128]{1,0:T(8,128)S(1)}, f32[1024,128]{1,0:T(8,128)S(1)}, u32[]{:S(2)}, u32[]{:S(2)}) collective-permute-start(f32[1024,128]{1,0:T(8,128)S(1)} %constant_dynamic-update-slice_fusion.5), channel_id=1, source_target_pairs={{0,16},{16,32},{32,48},{48,0},{1,17},{17,33},{33,49},{49,1},{2,18}... | collective-permute-start | bytes 1572872 | tf_op jit(solution)/shard_map/ppermute | solution.py:288
  115.8 7.8 %collective-permute-start.21 = (f32[512,128]{1,0:T(8,128)S(1)}, f32[512,128]{1,0:T(8,128)S(1)}, u32[]{:S(2)}, u32[]{:S(2)}) collective-permute-start(f32[512,128]{1,0:T(8,128)S(1)} %slice.49), channel_id=1, source_target_pairs={{0,192},{64,0},{128,64},{192,128},{1,193},{65,1},{129,65},{193,129... | collective-permute-start | bytes 786440 | tf_op jit(solution)/shard_map/ppermute | solution.py:288
  116.1 7.5 %collective-permute-start.20 = (f32[512,128]{1,0:T(8,128)S(1)}, f32[512,128]{1,0:T(8,128)}, u32[]{:S(2)}, u32[]{:S(2)}) collective-permute-start(f32[512,128]{1,0:T(8,128)S(1)} %slice.48), channel_id=1, source_target_pairs={{0,64},{64,128},{128,192},{192,0},{1,65},{65,129},{129,193},{193,1... | collective-permute-start | bytes 786440 | tf_op jit(solution)/shard_map/ppermute | solution.py:288
  119.4 6.6 %collective-permute-start.29 = (f32[512,128]{1,0:T(8,128)S(1)}, f32[512,128]{1,0:T(8,128)}, u32[]{:S(2)}, u32[]{:S(2)}) collective-permute-start(f32[512,128]{1,0:T(8,128)S(1)} %slice.54), channel_id=1, source_target_pairs={{0,48},{16,0},{32,16},{48,32},{1,49},{17,1},{33,17},{49,33},{2,50}... | collective-permute-start | bytes 786440 | tf_op jit(solution)/shard_map/ppermute | solution.py:288
  120.0 7.8 %collective-permute-start.28 = (f32[512,128]{1,0:T(8,128)S(1)}, f32[512,128]{1,0:T(8,128)}, u32[]{:S(2)}, u32[]{:S(2)}) collective-permute-start(f32[512,128]{1,0:T(8,128)S(1)} %slice.53), channel_id=1, source_target_pairs={{0,16},{16,32},{32,48},{48,0},{1,17},{17,33},{33,49},{49,1},{2,18}... | collective-permute-start | bytes 786440 | tf_op jit(solution)/shard_map/ppermute | solution.py:288
  123.6 4.1 %copy-start = (f32[512,128]{1,0:T(8,128)}, f32[512,128]{1,0:T(8,128)S(1)}, u32[]{:S(2)}) copy-start(f32[512,128]{1,0:T(8,128)S(1)} %collective-permute-done.21) | copy-start | bytes 786436
Sparse Core Ops, SparseCore 0:
  53.9 49.4 all-gather.2
